TPU v7x, 128 devices: a whole 4x4x4 slice. The times are simulated.
128 devices in a mesh: freq: 8 (over z_lo, y), band: 16 (over x, z_hi, core).
Axes of the slice: x: 4, y: 4, z: 4 (z_hi: 2, z_lo: 2; z = z_hi * 2 + z_lo), core: 2. Of those that a mesh axis runs over, the one named last changes fastest.
Arguments:
- pair_density: bfloat16 [4096, 2, 8192], P(('freq', 'band')), may hold values from -6 to 6
- trial_vectors: bfloat16 [32, 2, 64, 8192], P('freq', None, None, 'band'), may hold values from -6 to 6
- frequency: float32 [32], P('freq'), may hold values from 0.05 to 20
- val_energy: float32 [32], replicated, may hold values from -3 to -0.1
- cond_energy: float32 [128], replicated, may hold values from 0.1 to 4
- pair_index: int32 [4096], P(('freq', 'band')), may hold values from 0 to 4095, each once
Outputs:
- images: float32 [32, 2, 64, 8192], P('freq', None, None, 'band')
- subspace: float32 [32, 2, 64, 64], P('freq')
Inputs may be any that keep to these rules, and one draw needn't show every extreme that they name: `pair_index`: every pair number 0 to 4095 appears exactly once.
All inputs are finite; a program needn't handle non-finite values.
Results may differ from a plain program's by a relative error of at most 0.0085.
Values may be sent and summed in bfloat16 or wider, within the bound.
A program may use at most 128 MiB of HBM per device.

v0:
```python
import math

import jax
import jax.numpy as jnp
from jax import lax
from jax.sharding import PartitionSpec as P


def split_up(array, dim, size):
    before, after = (array.shape[:dim], array.shape[dim + 1 :])
    return jnp.moveaxis(array.reshape(*before, size, -1, *after), dim, 0)


def sent_and_summed(array, axis, dim):
    size = lax.axis_size(axis)
    parts = lax.all_to_all(split_up(array, dim, size), axis, 0, 0, tiled=True)
    return jnp.sum(parts.astype(jnp.float32), axis=0)


def copy_for_each(array, axis):
    size = lax.axis_size(axis)
    return lax.all_to_all(
        jnp.broadcast_to(array[None], (size, *array.shape)), axis, 0, 0, tiled=True
    )


def taken_together(array, axis):
    everything = copy_for_each(array, axis)
    return jnp.sum(everything, axis=0)


def local_weights(pair_index, frequency, val_energy, cond_energy, prefactor):
    cond_count = cond_energy.shape[0]
    val_count = val_energy.shape[0]
    cond_pick = jnp.sum(
        jnp.where(
            (pair_index % cond_count)[:, None] == jnp.arange(cond_count)[None, :],
            cond_energy[None, :],
            0.0,
        ),
        axis=1,
    )
    val_pick = jnp.sum(
        jnp.where(
            (pair_index // cond_count)[:, None] == jnp.arange(val_count)[None, :],
            val_energy[None, :],
            0.0,
        ),
        axis=1,
    )
    delta = cond_pick - val_pick
    ratio = delta[:, None] / (
        delta[:, None] * delta[:, None] + frequency[None, :] * frequency[None, :]
    )
    return (-4.0 * prefactor * ratio).astype(jnp.bfloat16)


def crossing_terms(density, vectors):
    products = jnp.einsum("pcg,fekg->fcekp", density, vectors, preferred_element_type=jnp.float32)
    return jnp.stack(
        [products[:, 0, 0] + products[:, 1, 1], products[:, 0, 1] - products[:, 1, 0]], 1
    )


def scale_terms(crossings, weights):
    factor = jnp.transpose(weights.astype(jnp.float32))[:, None, None, :]
    return (factor * crossings).astype(jnp.bfloat16)


def mix_terms(scaled):
    scaled_real = scaled[:, 0]
    scaled_imag = scaled[:, 1]
    return jnp.stack(
        [jnp.stack([scaled_real, -scaled_imag], 1), jnp.stack([scaled_imag, scaled_real], 1)], 1
    )


def image_terms(density, mixed):
    return jnp.einsum("pcg,fdckp->fdkg", density, mixed, preferred_element_type=jnp.float32)


def shards(pair_density, trial_vectors, frequency, val_energy, cond_energy, pair_index):
    groups = lax.axis_size("freq")
    members = lax.axis_size("band")
    pair_count = pair_density.shape[0] * groups * members
    grid_count = trial_vectors.shape[3] * members
    prefactor = 1.0 / math.sqrt(2.0 * grid_count * pair_count)
    gathered = lax.all_gather(trial_vectors, "band", axis=3, tiled=True)
    density = lax.all_gather(pair_density, "freq", axis=0, tiled=True)
    piece_index = lax.all_gather(pair_index, "freq", axis=0, tiled=True)
    piece_weights = local_weights(piece_index, frequency, val_energy, cond_energy, prefactor)
    scaled = scale_terms(crossing_terms(density, gathered), piece_weights)
    totals = image_terms(density, mix_terms(scaled))
    images = sent_and_summed(totals.astype(jnp.bfloat16), "band", 3)
    vectors = trial_vectors.astype(jnp.float32)
    highest = lax.Precision.HIGHEST
    real_part = jnp.einsum(
        "fkg,flg->fkl", vectors[:, 0], images[:, 0], precision=highest
    ) + jnp.einsum("fkg,flg->fkl", vectors[:, 1], images[:, 1], precision=highest)
    imag_part = jnp.einsum(
        "fkg,flg->fkl", vectors[:, 0], images[:, 1], precision=highest
    ) - jnp.einsum("fkg,flg->fkl", vectors[:, 1], images[:, 0], precision=highest)
    partial_value = jnp.stack([real_part, imag_part], 1) / grid_count
    subspace = taken_together(partial_value, "band")
    return (images, subspace)


def solution(mesh):
    return jax.shard_map(
        shards,
        mesh=mesh,
        in_specs=(
            P(("freq", "band"), None, None),
            P("freq", None, None, "band"),
            P("freq"),
            P(),
            P(),
            P(("freq", "band")),
        ),
        out_specs=(P("freq", None, None, "band"), P("freq", None, None, None)),
        check_vma=False,
    )
```

profile of v0, /device:TPU:0, one launch (start us, length us, event | category | flops | bytes accessed | tf_op | source)
XLA Modules:
  0.0 373.4 jit_solution(17423655233656940172)
XLA Ops:
  7.2 0.0 all-gather.5.cloned.1.call-start
  7.2 2.8 copy.27
  10.0 0.0 all-gather.5.cloned.1.call-update
  10.0 0.0 all-gather.3.cloned.1.call-start
  10.1 0.7 all-gather.3.cloned.1.call-update
  10.8 0.7 mul.32
  11.5 1.2 dynamic-slice
  13.4 0.9 dynamic-update-slice
  14.3 13.1 %all-reduce = s32[256]{0:T(256)S(1)} all-reduce(s32[256]{0:T(256)S(1)} %dynamic-update-slice), channel_id=1, replica_groups=mesh['freq'=8,'band'=16] {'freq'}, use_global_device_ids=true, to_apply=%add | all-reduce | flops 256 | bytes 2048
  27.3 0.7 select_reduce_fusion.1
  28.1 0.8 select_reduce_fusion
  28.9 0.1 fusion.26
  29.0 75.7 %all-gather.5.cloned.1.call-done = bf16[256,2,8192]{2,0,1:T(8,128)(2,1)} async-done(((bf16[32,2,8192]{2,0,1:T(8,128)(2,1)}), bf16[256,2,8192]{2,0,1:T(8,128)(2,1)}) %all-gather.5.cloned.1.call-update) | async-done | bytes 8388624 | tf_op jit(solution)/shard_map/all_gather | solution.py:89
  104.7 80.1 %all-gather.3.cloned.1.call-done = bf16[4,2,64,8192]{3,2,1,0:T(8,128)(2,1)} async-done(((bf16[4,2,64,512]{3,2,1,0:T(8,128)(2,1)}), bf16[4,2,64,8192]{3,2,1,0:T(8,128)(2,1)}) %all-gather.3.cloned.1.call-update) | async-done | bytes 8388624 | tf_op jit(solution)/shard_map/all_gather | solution.py:88
  184.8 9.6 %fusion.4 = f32[4,2,2,64,256]{4,3,1,2,0:T(8,128)S(1)} fusion(bf16[256,2,8192]{2,0,1:T(8,128)(2,1)} %all-gather.5.cloned.1.call-done, bf16[4,2,64,8192]{3,2,1,0:T(8,128)(2,1)} %all-gather.3.cloned.1.call-done), kind=kOutput, calls=%fused_computation.7 | convolution fusion | flops 4294967296 | bytes 17825792 | tf_op jit(solution)/shard_map/pcg,fekg->fcekp/dot_general | solution.py:59
  194.6 6.8 %bitcast_convert_fusion = bf16[4,2,64,8192]{3,2,1,0:T(8,128)(2,1)} fusion(bf16[256,2,8192]{2,0,1:T(8,128)(2,1)S(1)} %copy-done.2, bf16[4,1,2,64,256]{4,3,0,2,1:T(8,128)(2,1)S(1)} %get-tuple-element.10, bf16[4,1,2,64,256]{4,3,0,2,1:T(8,128)(2,1)S(1)} %get-tuple-element.9), kind=kOutput, calls=%fused_computation | convolution fusion | flops 4299423744 | bytes 17301504 | tf_op jit(solution)/shard_map/pcg,fdckp->fdkg/dot_general | solution.py:79
  201.4 7.9 %copy.52 = bf16[4,2,8,16,8,512]{5,4,2,1,0,3:T(8,128)(2,1)} copy(bf16[4,2,8,16,8,512]{5,4,3,2,1,0:T(8,128)(2,1)} %bitcast.82) | data formatting | bytes 16777216 | tf_op jit(solution)/shard_map/reshape | solution.py:11
  209.3 100.4 %all_to_all.10 = bf16[16,4,2,64,512]{4,3,2,1,0:T(8,128)(2,1)S(1)} all-to-all(bf16[16,4,2,64,512]{4,3,2,1,0:T(8,128)(2,1)} %bitcast.81), channel_id=1, replica_groups=mesh['freq'=8,'band'=16] {'band'}, dimensions={0} | all-to-all | bytes 16777216 | tf_op jit(solution)/shard_map/all_to_all | solution.py:16
  309.7 1.5 convert_reduce_fusion
  311.2 0.0 copy-start
  311.3 0.4 fusion.14
  311.6 0.4 fusion.13
  312.0 0.4 fusion.9
  312.4 0.4 fusion.10
  312.8 0.1 copy.37
  312.9 2.5 broadcast_in_dim.30
  315.4 4.5 %reshape.125 = f32[16,1,32768]{2,1,0:T(1,128)S(1)} reshape(f32[16,4,2,64,64]{4,3,2,1,0:T(8,128)} %broadcast_in_dim.30) | data formatting | bytes 4194304
  319.9 32.5 %all_to_all.11 = f32[16,1,32768]{2,1,0:T(1,128)} all-to-all(f32[16,1,32768]{2,1,0:T(1,128)S(1)} %reshape.125), channel_id=1, replica_groups=mesh['freq'=8,'band'=16] {'band'}, dimensions={0} | all-to-all | bytes 4194304 | tf_op jit(solution)/shard_map/all_to_all | solution.py:22
  352.4 0.5 broadcast.72
  352.9 7.3 %reduce = f32[16,32768]{1,0:T(8,128)S(1)} reduce(f32[16,1,32768]{2,1,0:T(1,128)} %all_to_all.11, f32[]{:T(128)} %broadcast.72), dimensions={1}, to_apply=%all_to_all.7.reduce_sub_computation | reduce | bytes 4194308 | tf_op jit(solution)/shard_map/all_to_all | solution.py:22
  360.2 3.0 reshape.126
  363.2 3.4 reduce_sum.39
  (14 shorter events, 0.2 us)
Async XLA Ops:
  7.2 97.5 %all-gather.5.cloned.1.call-start = ((), (), s32[]{:S(2)}) async-start(), calls=%async_computation.3 | async-start | bytes 9437184 | tf_op jit(solution)/shard_map/all_gather | solution.py:89
  10.0 174.8 %all-gather.3.cloned.1.call-start = ((), (), s32[]{:S(2)}) async-start(), calls=%async_computation.2 | async-start | bytes 8912896 | tf_op jit(solution)/shard_map/all_gather | solution.py:88
  184.8 9.8 %copy-start.2 = (bf16[256,2,8192]{2,0,1:T(8,128)(2,1)S(1)}, bf16[256,2,8192]{2,0,1:T(8,128)(2,1)}, u32[]{:S(2)}) copy-start(bf16[256,2,8192]{2,0,1:T(8,128)(2,1)} %all-gather.5.cloned.1.call-done) | copy-start | bytes 25165828
  309.7 1.6 copy-start.1
  311.2 41.2 %copy-start = (f32[4,2,64,512]{3,2,1,0:T(8,128)}, f32[4,2,64,512]{3,2,1,0:T(8,128)S(1)}, u32[]{:S(2)}) copy-start(f32[4,2,64,512]{3,2,1,0:T(8,128)S(1)} %convert_reduce_fusion) | copy-start | bytes 3145732
Sparse Core Ops, SparseCore 0:
  10.2 94.4 all-gather.4
  107.0 77.8 all-gather.2
where the time goes:
time: 374 us; the launch traced here: 373 us
  waiting for transfers between devices  157 us (42%)
  blocking collectives  146 us (39%)
  local copies, waits for them, and re-layouts  23.4 us (6%)
  matrix products  17.8 us (5%)
  between operations  14.9 us (4%)
  other arithmetic  14.8 us (4%)
    all_to_all x1, blocking collectives, sent_and_summed(): parts = lax.all_to_all(split_up(array, dim, size), axis, 0, 0, tiled=True)  100 us
    all_gather x1, waiting for transfers between devices, shards(): gathered = lax.all_gather(trial_vectors, 'band', axis=3, tiled=True)  80.1 us
    all_gather x1, waiting for transfers between devices, shards(): density = lax.all_gather(pair_density, 'freq', axis=0, tiled=True)  75.7 us
    all_to_all x1, blocking collectives, copy_for_each(): lax.all_to_all(jnp.broadcast_to(array[None], (size, *array.shape)), axis,...  32.5 us
    unnamed x1, blocking collectives  13.1 us
    unnamed x12, local copies, waits for them, and re-layouts  12.4 us
    dot_general x1, matrix products, crossing_terms(): jnp.einsum('pcg,fekg->fcekp', density, vectors, preferred_element_type=jn...  9.55 us
    reshape x1, local copies, waits for them, and re-layouts, split_up(): return jnp.moveaxis(array.reshape(*before, size, -1, *after), dim, 0)  7.88 us
  transfers between devices with their start and end apart: 2, of which 2 were waited for; matrix products, arithmetic and copies ran while one was open for 1% of the time, Pallas kernels for 0%

commit v1 on v0

v1 whole, which is shorter than its diff:
```python
import functools
import math

import jax
import jax.numpy as jnp
from jax import lax
from jax.experimental import pallas as pl
from jax.experimental.pallas import tpu as pltpu
from jax.sharding import PartitionSpec as P

MESH = pl.DeviceIdType.MESH
ORDER = (0, 1, 3, 2)


def wrap(v, n=4):
    return lax.rem(v + n, n)


def dev(x, y, z, c):
    x, y, z, c = wrap(x), wrap(y), wrap(z), wrap(c, 2)
    return (lax.rem(z, 2) * 4 + y, x * 4 + (z // 2) * 2 + c)


def dot_nt(a, b):
    return lax.dot_general(a, b, (((1,), (1,)), ((), ())), preferred_element_type=jnp.float32)


def kernel(
    consts,
    rho, xin, idx, cond, val, freq,
    img, sub,
    R, XF, acc, C32, CB, CR, SF, L, SB, RI, D, SZ, SO, SA, FQ,
    x_s, x_r, y_s, y_r, f_s, f_r, p_s, p_r, v_s, v_r, c_s, c_r, g_s, g_r,
    i_s, i_r, d_s, d_r, u_s, u_r, w_s, w_r, q_s, q_r,
):
    prefactor, grid_count = consts
    fi, bi = lax.axis_index("freq"), lax.axis_index("band")
    zl, y = fi // 4, lax.rem(fi, 4)
    x, zh, c = bi // 4, lax.rem(bi // 2, 2), lax.rem(bi, 2)
    z = zh * 2 + zl
    me = (fi, bi)
    partner = dev(x, y, z, 1 - c)
    aligned = zl == c
    pending = []

    def send(src, dst, ss, rs, to):
        copy = pltpu.make_async_remote_copy(
            src_ref=src, dst_ref=dst, send_sem=ss, recv_sem=rs, device_id=to, device_id_type=MESH
        )
        copy.start()
        return copy

    def keep(copy):
        pending.append(copy)

    def arrived(dst, rs):
        pltpu.make_async_remote_copy(
            src_ref=dst, dst_ref=dst, send_sem=rs, recv_sem=rs, device_id=me, device_id_type=MESH
        ).wait_recv()

    def sent(src, ss):
        pltpu.make_async_remote_copy(
            src_ref=src, dst_ref=src, send_sem=ss, recv_sem=ss, device_id=me, device_id_type=MESH
        ).wait_send()

    plane = [
        (dy, dx, cc) for dy in range(4) for dx in range(4) for cc in range(2) if (dy, dx, cc) != (0, 0, 0)
    ]
    barrier = pltpu.get_barrier_semaphore()
    for dy, dx, cc in plane:
        pl.semaphore_signal(barrier, inc=1, device_id=dev(x + dx, y + dy, z, c + cc), device_id_type=MESH)
    for dz in (1, 2, 3):
        for cc in range(2):
            pl.semaphore_signal(barrier, inc=1, device_id=dev(x, y, z + dz, cc), device_id_type=MESH)

    lane = lax.broadcasted_iota(jnp.int32, (8, 128), 1)
    lane32 = jnp.bitwise_and(lane, 31)
    number = jnp.zeros((8, 128), jnp.int32)
    for i in range(32):
        number = jnp.where(lane32 == i, idx[i], number)
    cond_no = jnp.bitwise_and(number, 127)
    val_no = jnp.right_shift(number, 7)
    zero = jnp.zeros((8, 128), jnp.float32)
    cond_pick = lax.fori_loop(0, 128, lambda j, a: jnp.where(cond_no == j, cond[j], a), zero)
    val_pick = lax.fori_loop(0, 32, lambda j, a: jnp.where(val_no == j, val[j], a), zero)
    mine = jnp.right_shift(lane, 5) == lax.rem(x, 2) * 2 + c
    D[x * 2 + c] = jnp.where(mine, cond_pick - val_pick, 0.0)
    R[0, :, x, c] = rho[x]

    def lanes(block):
        return pl.ds(pl.multiple_of(block * 512, 512), 512)

    for f in range(4):
        FQ[0, f] = jnp.full((8, 128), freq[f], jnp.float32)

    @pl.when(aligned)
    def _():
        XF[:, :, :, lanes(zh * 2 + c)] = xin[...]
        FQ[1] = FQ[0]

    pl.semaphore_wait(barrier, len(plane) + 6)

    def at(e):
        return wrap(x - e)

    def spread(e):
        src = rho.at[x] if e == 0 else R.at[0, :, at(e), c]
        keep(send(src, R.at[1, :, at(e), c], y_s.at[0, e], y_r.at[0, e], dev(x, y + 1, z, c)))
        keep(send(src, R.at[3, :, at(e), c], y_s.at[1, e], y_r.at[1, e], dev(x, y - 1, z, c)))
        keep(send(src, R.at[0, :, at(e), c], p_s.at[0, e], p_r.at[0, e], partner))

    def pass_on(e):
        arrived(R.at[1, :, at(e), c], y_r.at[0, e])
        keep(send(R.at[1, 0, at(e), c], R.at[2, 0, at(e), c], f_s.at[0, e], f_r.at[0, e], dev(x, y + 1, z, c)))
        keep(send(R.at[1, :, at(e), c], R.at[1, :, at(e), c], p_s.at[1, e], p_r.at[1, e], partner))
        arrived(R.at[3, :, at(e), c], y_r.at[1, e])
        keep(send(R.at[3, 1, at(e), c], R.at[2, 1, at(e), c], f_s.at[1, e], f_r.at[1, e], dev(x, y - 1, z, c)))
        keep(send(R.at[3, :, at(e), c], R.at[3, :, at(e), c], p_s.at[3, e], p_r.at[3, e], partner))

    def pass_far(e):
        arrived(R.at[2, 0, at(e), c], f_r.at[0, e])
        arrived(R.at[2, 1, at(e), c], f_r.at[1, e])
        keep(send(R.at[2, :, at(e), c], R.at[2, :, at(e), c], p_s.at[2, e], p_r.at[2, e], partner))

    def partner_done(dy):
        for e in ORDER:
            arrived(R.at[dy, :, at(e), 1 - c], p_r.at[dy, e])

    for e in (1, 3, 2):
        keep(send(rho.at[wrap(x + e)], R.at[0, :, x, c], x_s.at[e], x_r.at[e], dev(x + e, y, z, c)))
    spread(0)
    my_lanes = lanes(zh * 2 + c)
    for dz in (1, 3, 2):
        keep(send(xin, XF.at[:, :, :, my_lanes], v_s.at[dz], v_r.at[dz, c], dev(x, y, z + dz, zl)))

    @pl.when(jnp.logical_not(aligned))
    def _():
        send(xin, XF.at[:, :, :, my_lanes], v_s.at[0], v_r.at[0, c], partner)

    @pl.when(aligned)
    def _():
        send(FQ.at[0], FQ.at[1], q_s, q_r, dev(x, y, z - 1, c))

    for dy, dx, cc in plane:
        send(D.at[x * 2 + c], D.at[dy * 8 + x * 2 + c], d_s, d_r, dev(x + dx, y + dy, z, c + cc))

    def vectors_done():
        @pl.when(aligned)
        def _():
            arrived(XF.at[:, :, :, lanes(zh * 2 + 1 - c)], v_r.at[0, 1 - c])
            for cc in range(2):
                arrived(XF.at[:, :, :, lanes((1 - zh) * 2 + cc)], v_r.at[2, cc])

        @pl.when(jnp.logical_not(aligned))
        def _():
            for dz in (1, 3):
                for cc in range(2):
                    arrived(XF.at[:, :, :, lanes((wrap(z - dz) // 2) * 2 + cc)], v_r.at[dz, cc])

    def cross(dy):
        v = XF[...].reshape(512, 2048)
        t_re = dot_nt(v, R[dy, 0].reshape(256, 2048)).reshape(4, 2, 64, 256)
        t_im = dot_nt(v, R[dy, 1].reshape(256, 2048)).reshape(4, 2, 64, 256)
        re = t_re[:, 0] + t_im[:, 1]
        im = t_re[:, 1] - t_im[:, 0]
        C32[dy, :, 0] = re
        C32[dy, :, 1] = im
        CB[dy, :, 0] = re.astype(jnp.bfloat16)
        CB[dy, :, 1] = im.astype(jnp.bfloat16)
        for e in (1, 3, 2):
            keep(send(CB.at[dy, wrap(x + e)], CR.at[dy, e], c_s.at[dy, e], c_r.at[dy, e], dev(x + e, y, z, c)))

    def scale(dy):
        total = C32[dy, x]
        for e in (1, 2, 3):
            arrived(CR.at[dy, e], c_r.at[dy, e])
        for e in (1, 2, 3):
            total = total + CR[dy, e].astype(jnp.float32)
        halves = []
        for h in range(2):
            first = dy * 8 + h * 4
            halves.append(D[first] + D[first + 1] + D[first + 2] + D[first + 3])
        delta = jnp.concatenate(halves, axis=1)[0:1]
        own = FQ[1, x][0:1, 0:1]
        ratio = delta / (delta * delta + own * own)
        weight = (-4.0 * prefactor * ratio).astype(jnp.bfloat16).astype(jnp.float32)
        scaled = (weight[None] * total).astype(jnp.bfloat16)
        SF[dy, x] = scaled
        for e in (1, 3, 2):
            keep(send(SF.at[dy, x], SF.at[dy, x], g_s.at[dy, e], g_r.at[dy, e], dev(x + e, y, z, c)))
        flat = total.reshape(128, 256)
        high = flat.astype(jnp.bfloat16)
        low = (flat - high.astype(jnp.float32)).astype(jnp.bfloat16)
        part = dot_nt(jnp.concatenate([high, low], axis=0), scaled.reshape(128, 256))
        if dy == 0:
            SA[...] = part
        else:
            SA[...] += part

    def gathered(dy):
        for e in (1, 3, 2):
            arrived(SF.at[dy, at(e)], g_r.at[dy, e])
        re, im = SF[dy, :, 0], SF[dy, :, 1]
        L[:, 0, :, 0:256] = re
        L[:, 0, :, 256:512] = -im
        L[:, 1, :, 0:256] = im
        L[:, 1, :, 256:512] = re

    def image_tile(dy, block):
        at_lanes = lanes(block)
        return jnp.dot(
            L[...].reshape(512, 512),
            R[dy, :, :, :, :, at_lanes].reshape(512, 512),
            preferred_element_type=jnp.float32,
        )

    def image(dy):
        gathered(dy)

        @pl.loop(0, 4)
        def _(block):
            part = image_tile(dy, block)
            if dy == 0:
                acc[:, lanes(block)] = part
            else:
                acc[:, lanes(block)] += part

    for e in (1, 3):
        arrived(R.at[0, :, at(e), c], x_r.at[e])
        spread(e)
    pass_on(0)
    arrived(R.at[0, :, at(2), c], x_r.at[2])
    spread(2)
    pass_on(1)
    pass_on(3)
    vectors_done()
    partner_done(0)
    cross(0)
    pass_on(2)
    partner_done(1)
    cross(1)
    partner_done(3)
    cross(3)
    most = D.at[pl.ds(0, 31)]
    arrived(most, d_r)
    sent(most, d_s)

    @pl.when(aligned)
    def _():
        sent(FQ.at[0], q_s)

    @pl.when(jnp.logical_not(aligned))
    def _():
        arrived(FQ.at[1], q_r)

    scale(0)
    scale(1)
    scale(3)
    pass_far(0)
    image(0)
    pass_far(1)
    image(1)
    pass_far(3)
    image(3)
    pass_far(2)
    partner_done(2)
    cross(2)
    scale(2)

    both = SA[0:128] + SA[128:256]
    re = both[0:64, 0:64] + both[64:128, 64:128]
    im = both[0:64, 64:128] - both[64:128, 0:64]
    mine_sub = jnp.concatenate([re, im], axis=1) / grid_count

    gathered(2)
    for step in range(4):
        h = 1 - zh if step < 2 else zh
        cc = 1 - c if step % 2 == 0 else c
        block = h * 2 + cc
        total = acc[:, lanes(block)] + image_tile(2, block)
        to_z = h * 2 + c
        dz = wrap(to_z - z)
        half = total.astype(jnp.bfloat16).reshape(4, 2, 64, 512)
        if step < 3:
            SB[step] = half
            keep(send(SB.at[step], RI.at[dz], i_s.at[step], i_r.at[dz], dev(x, y, to_z, cc)))
        else:
            SB[step] = half

            @pl.when(jnp.logical_not(aligned))
            def _():
                send(SB.at[3], RI.at[dz], i_s.at[3], i_r.at[dz], dev(x, y, to_z, cc))

            @pl.when(aligned)
            def _():
                RI[0] = half

    return_sub(
        mine_sub, sub, SZ, SO, x, y, z, zh, c, aligned, send, keep, arrived, sent, u_s, u_r, w_s, w_r, at
    )

    for dz in (1, 3, 2):
        arrived(RI.at[dz], i_r.at[dz])

    @pl.when(jnp.logical_not(aligned))
    def _():
        arrived(RI.at[0], i_r.at[0])

    @pl.loop(0, 4)
    def _(f):
        total = RI[0, f].astype(jnp.float32)
        for dz in (1, 2, 3):
            total = total + RI[dz, f].astype(jnp.float32)
        img[f] = total

    for copy in pending:
        copy.wait_send()

    @pl.when(jnp.logical_not(aligned))
    def _():
        sent(xin, v_s.at[0])
        sent(SB.at[3], i_s.at[3])


def return_sub(mine_sub, sub, SZ, SO, x, y, z, zh, c, aligned, send, keep, arrived, sent, u_s, u_r, w_s, w_r, at):
    SZ[0] = mine_sub

    @pl.when(aligned)
    def _():
        SZ[1 + z] = mine_sub
        send(SZ.at[0], SZ.at[1 + z], u_s.at[0], u_r.at[2], dev(x, y, z + 2, c))
        for dz in (1, 3, 2):
            arrived(SZ.at[1 + wrap(z - dz)], u_r.at[dz])
        SO[x] = SZ[1] + SZ[2] + SZ[3] + SZ[4]
        for e in (1, 3, 2):
            for cc in range(2):
                send(SO.at[x], SO.at[x], w_s.at[e, cc], w_r.at[e], dev(x + e, y, z, cc))
        send(SO.at[x], SO.at[x], w_s.at[0, 0], w_r.at[0], dev(x, y, z, 1 - c))
        sent(SZ.at[0], u_s.at[0])
        for e in (1, 3, 2):
            for cc in range(2):
                sent(SO.at[x], w_s.at[e, cc])
        sent(SO.at[x], w_s.at[0, 0])

    @pl.when(jnp.logical_not(aligned))
    def _():
        for k, dz in enumerate((1, 3)):
            send(SZ.at[0], SZ.at[1 + z], u_s.at[k], u_r.at[dz], dev(x, y, z + dz, c))
        for k in range(2):
            sent(SZ.at[0], u_s.at[k])
        arrived(SO.at[x], w_r.at[0])

    for e in (1, 3, 2):
        arrived(SO.at[at(e)], w_r.at[e])
    for f in range(4):
        both = SO[f]
        sub[f, 0] = both[:, 0:64]
        sub[f, 1] = both[:, 64:128]


def shards(pair_density, trial_vectors, frequency, val_energy, cond_energy, pair_index):
    groups = lax.axis_size("freq")
    members = lax.axis_size("band")
    pair_count = pair_density.shape[0] * groups * members
    grid_count = trial_vectors.shape[3] * members
    prefactor = 1.0 / math.sqrt(2.0 * grid_count * pair_count)
    pieces = jnp.transpose(pair_density.reshape(32, 2, 4, 2048), (2, 1, 0, 3))
    bf, f32 = jnp.bfloat16, jnp.float32
    vmem = pl.BlockSpec(memory_space=pltpu.VMEM)
    smem = pl.BlockSpec(memory_space=pltpu.SMEM)
    dma = pltpu.SemaphoreType.DMA
    return pl.pallas_call(
        functools.partial(kernel, (prefactor, grid_count)),
        name="response",
        out_shape=(
            jax.ShapeDtypeStruct((4, 2, 64, 512), f32),
            jax.ShapeDtypeStruct((4, 2, 64, 64), f32),
        ),
        in_specs=[vmem, vmem, smem, smem, smem, smem],
        out_specs=(vmem, vmem),
        scratch_shapes=[
            pltpu.VMEM((4, 2, 4, 2, 32, 2048), bf),
            pltpu.VMEM((4, 2, 64, 2048), bf),
            pltpu.VMEM((512, 2048), f32),
            pltpu.VMEM((4, 4, 2, 64, 256), f32),
            pltpu.VMEM((4, 4, 2, 64, 256), bf),
            pltpu.VMEM((4, 4, 2, 64, 256), bf),
            pltpu.VMEM((4, 4, 2, 64, 256), bf),
            pltpu.VMEM((4, 2, 64, 512), bf),
            pltpu.VMEM((4, 4, 2, 64, 512), bf),
            pltpu.VMEM((4, 4, 2, 64, 512), bf),
            pltpu.VMEM((32, 8, 128), f32),
            pltpu.VMEM((5, 64, 128), f32),
            pltpu.VMEM((4, 64, 128), f32),
            pltpu.VMEM((256, 128), f32),
            pltpu.VMEM((2, 4, 8, 128), f32),
            dma((4,)), dma((4,)),
            dma((2, 4)), dma((2, 4)),
            dma((2, 4)), dma((2, 4)),
            dma((4, 4)), dma((4, 4)),
            dma((4,)), dma((4, 2)),
            dma((4, 4)), dma((4, 4)),
            dma((4, 4)), dma((4, 4)),
            dma((4,)), dma((4,)),
            dma, dma,
            dma((2,)), dma((4,)),
            dma((4, 2)), dma((4,)),
            dma, dma,
        ],
        compiler_params=pltpu.CompilerParams(
            collective_id=0, has_side_effects=True, vmem_limit_bytes=56 * 2**20
        ),
    )(pieces, trial_vectors, pair_index, cond_energy, val_energy, frequency)


def solution(mesh):
    return jax.shard_map(
        shards,
        mesh=mesh,
        in_specs=(
            P(("freq", "band"), None, None),
            P("freq", None, None, "band"),
            P("freq"),
            P(),
            P(),
            P(("freq", "band")),
        ),
        out_specs=(P("freq", None, None, "band"), P("freq", None, None, None)),
        check_vma=False,
    )
```

time: 374 us -> 122 us (0.33)
  waiting for transfers between devices: 157 us -> 0 us
  blocking collectives: 146 us -> 0 us
  Pallas kernels: 0 us -> 114 us
  matrix products: 17.8 us -> 0 us
  local copies, waits for them, and re-layouts: 23.4 us -> 6.3 us
  other arithmetic: 14.8 us -> 0 us
  between operations: 14.9 us -> 0.65 us
    all_gather x2 -> x0, waiting for transfers between devices: 156 us -> none  [the longest x1 80.1 us: shards(): gathered = lax.all_gather(trial_vectors, 'band', axis=3, tiled=True)]
    all_to_all x2 -> x0, blocking collectives: 133 us -> none  [the longest x1 100 us: sent_and_summed(): parts = lax.all_to_all(split_up(array, dim, size), axis, 0, 0, tiled=True)]
    pallas_call x0 -> x1, Pallas kernels: none -> 114 us  [shards(): pl.pallas_call(functools.partial(kernel, (prefactor, grid_count)), name='...]
    dot_general x6 -> x0, matrix products: 17.8 us -> none  [the longest x1 9.55 us: crossing_terms(): jnp.einsum('pcg,fekg->fcekp', density, vectors, preferred_element_type=jn...]
    unnamed x1 -> x0, blocking collectives: 13.1 us -> none
    unnamed x12 -> x4, local copies, waits for them, and re-layouts: 12.4 us -> 3.01 us
    all_to_all x1 -> x0, other arithmetic: 7.29 us -> none  [copy_for_each(): lax.all_to_all(jnp.broadcast_to(array[None], (size, *array.shape)), axis,...]
    reduce_sum x4 -> x0, other arithmetic: 6.5 us -> none  [the longest x1 3.38 us: taken_together(): return jnp.sum(everything, axis=0)]
  transfers between devices with their start and end apart: 2 -> 0, of which waited for: 2 -> 0; matrix products, arithmetic and copies ran while one was open for 1% -> 0% of each run, Pallas kernels for 0% -> 0%
where the time goes in v1:
time: 122 us; the launch traced here: 121 us
  Pallas kernels  114 us (93%)
  local copies, waits for them, and re-layouts  6.3 us (5%)
    pallas_call x1, Pallas kernels, shards(): pl.pallas_call(functools.partial(kernel, (prefactor, grid_count)), name='...  114 us
    reshape x2, local copies, waits for them, and re-layouts, shards(): pieces = jnp.transpose(pair_density.reshape(32, 2, 4, 2048), (2, 1, 0, 3))  3.29 us
    unnamed x4, local copies, waits for them, and re-layouts  3.01 us

profile of v1, /device:TPU:0, one launch (start us, length us, event | category | flops | bytes accessed | tf_op | source)
XLA Modules:
  0.0 120.5 jit_solution(4829737913679690446)
XLA Ops:
  0.6 1.7 %reshape.8 = bf16[32,2,4,2048]{3,2,1,0:T(4,128)(2,1)S(1)} reshape(bf16[32,2,8192]{2,1,0:T(2,128)(2,1)} %param.6) | data formatting | bytes 2097152 | tf_op jit(solution)/shard_map/reshape | solution.py:367
  2.4 1.5 %copy.13 = bf16[32,2,4,2048]{3,0,1,2:T(8,128)(2,1)} copy(bf16[32,2,4,2048]{3,2,1,0:T(4,128)(2,1)S(1)} %reshape.8) | data formatting | bytes 2097152 | tf_op jit(solution)/shard_map/reshape | solution.py:367
  3.9 113.6 %response.1 = (f32[4,2,64,512]{3,2,1,0:T(8,128)}, f32[4,2,64,64]{3,2,1,0:T(8,128)}) custom-call(bf16[4,2,32,2048]{3,2,1,0:T(8,128)(2,1)} %bitcast.3, bf16[4,2,64,512]{3,2,1,0:T(8,128)(2,1)} %xin.1, s32[32]{0:T(128)} %idx.1, f32[128]{0:T(128)} %cond.1, f32[32]{0:T(128)} %val.1, f32[4]{0:T(128)} %freq.1), custom_call_target="tpu_custom_call" | custom-call | tf_op jit(solution)/shard_map/response/pallas_call | solution.py:372
  117.5 0.0 copy-start
  117.5 2.3 %copy.16 = f32[4,2,64,512]{3,2,1,0:T(8,128)} copy(f32[4,2,64,512]{3,2,1,0:T(8,128)} %get-tuple-element.4) | data formatting | bytes 2097152
  119.8 0.0 copy-done
  119.8 0.7 copy.17
Async XLA Ops:
  117.5 2.3 %copy-start = (f32[4,2,64,64]{3,2,1,0:T(8,128)S(1)}, f32[4,2,64,64]{3,2,1,0:T(8,128)}, u32[]{:S(2)}) copy-start(f32[4,2,64,64]{3,2,1,0:T(8,128)} %get-tuple-element.5) | copy-start | bytes 393220

commit v2 on v1

--- a/solution.py
+++ b/solution.py
@@ -29,9 +29,9 @@
     consts,
     rho, xin, idx, cond, val, freq,
     img, sub,
-    R, XF, acc, C32, CB, CR, SF, L, SB, RI, D, SZ, SO, SA, FQ,
+    R, XF, acc, C32, CB, CR, SF, L, SB, RI, RC, D, SZ, SO, SA, FQ,
     x_s, x_r, y_s, y_r, f_s, f_r, p_s, p_r, v_s, v_r, c_s, c_r, g_s, g_r,
-    i_s, i_r, d_s, d_r, u_s, u_r, w_s, w_r, q_s, q_r,
+    i_s, i_r, k_r, d_s, d_r, u_s, u_r, w_s, w_r, q_s, q_r,
 ):
     prefactor, grid_count = consts
     fi, bi = lax.axis_index("freq"), lax.axis_index("band")
@@ -41,6 +41,7 @@
     me = (fi, bi)
     partner = dev(x, y, z, 1 - c)
     aligned = zl == c
+    unaligned = jnp.logical_not(aligned)
     pending = []
 
     def send(src, dst, ss, rs, to):
@@ -98,7 +99,8 @@
         XF[:, :, :, lanes(zh * 2 + c)] = xin[...]
         FQ[1] = FQ[0]
 
-    pl.semaphore_wait(barrier, len(plane) + 6)
+    with jax.named_scope("entry"):
+        pl.semaphore_wait(barrier, len(plane) + 6)
 
     def at(e):
         return wrap(x - e)
@@ -133,7 +135,7 @@
     for dz in (1, 3, 2):
         keep(send(xin, XF.at[:, :, :, my_lanes], v_s.at[dz], v_r.at[dz, c], dev(x, y, z + dz, zl)))
 
-    @pl.when(jnp.logical_not(aligned))
+    @pl.when(unaligned)
     def _():
         send(xin, XF.at[:, :, :, my_lanes], v_s.at[0], v_r.at[0, c], partner)
 
@@ -151,7 +153,7 @@
             for cc in range(2):
                 arrived(XF.at[:, :, :, lanes((1 - zh) * 2 + cc)], v_r.at[2, cc])
 
-        @pl.when(jnp.logical_not(aligned))
+        @pl.when(unaligned)
         def _():
             for dz in (1, 3):
                 for cc in range(2):
@@ -225,137 +227,190 @@
             else:
                 acc[:, lanes(block)] += part
 
-    for e in (1, 3):
+    def stage(name, fn, *args):
+        with jax.named_scope(name):
+            fn(*args)
+
+    def from_x(e):
         arrived(R.at[0, :, at(e), c], x_r.at[e])
         spread(e)
-    pass_on(0)
-    arrived(R.at[0, :, at(2), c], x_r.at[2])
-    spread(2)
-    pass_on(1)
-    pass_on(3)
-    vectors_done()
-    partner_done(0)
-    cross(0)
-    pass_on(2)
-    partner_done(1)
-    cross(1)
-    partner_done(3)
-    cross(3)
-    most = D.at[pl.ds(0, 31)]
-    arrived(most, d_r)
-    sent(most, d_s)
-
-    @pl.when(aligned)
-    def _():
-        sent(FQ.at[0], q_s)
-
-    @pl.when(jnp.logical_not(aligned))
-    def _():
-        arrived(FQ.at[1], q_r)
-
-    scale(0)
-    scale(1)
-    scale(3)
-    pass_far(0)
-    image(0)
-    pass_far(1)
-    image(1)
-    pass_far(3)
-    image(3)
-    pass_far(2)
-    partner_done(2)
-    cross(2)
-    scale(2)
-
-    both = SA[0:128] + SA[128:256]
-    re = both[0:64, 0:64] + both[64:128, 64:128]
-    im = both[0:64, 64:128] - both[64:128, 0:64]
-    mine_sub = jnp.concatenate([re, im], axis=1) / grid_count
-
-    gathered(2)
-    for step in range(4):
+
+    def energies_done():
+        most = D.at[pl.ds(0, 31)]
+        arrived(most, d_r)
+        sent(most, d_s)
+
+        @pl.when(aligned)
+        def _():
+            sent(FQ.at[0], q_s)
+
+        @pl.when(unaligned)
+        def _():
+            arrived(FQ.at[1], q_r)
+
+    stage("x1", from_x, 1)
+    stage("x3", from_x, 3)
+    stage("pass0", pass_on, 0)
+    stage("x2", from_x, 2)
+    stage("pass1", pass_on, 1)
+    stage("pass3", pass_on, 3)
+    stage("vectors", vectors_done)
+    stage("partner0", partner_done, 0)
+    stage("cross0", cross, 0)
+    stage("pass2", pass_on, 2)
+    stage("partner1", partner_done, 1)
+    stage("cross1", cross, 1)
+    stage("partner3", partner_done, 3)
+    stage("cross3", cross, 3)
+    stage("far0", pass_far, 0)
+    stage("energies", energies_done)
+    stage("scale0", scale, 0)
+    stage("far1", pass_far, 1)
+    stage("far3", pass_far, 3)
+    stage("scale1", scale, 1)
+    stage("far2", pass_far, 2)
+    stage("partner2", partner_done, 2)
+    stage("cross2", cross, 2)
+    stage("scale3", scale, 3)
+    stage("image0", image, 0)
+    stage("image1", image, 1)
+    stage("scale2", scale, 2)
+
+    def project_z():
+        both = SA[0:128] + SA[128:256]
+        re = both[0:64, 0:64] + both[64:128, 64:128]
+        im = both[0:64, 64:128] - both[64:128, 0:64]
+        SZ[z] = jnp.concatenate([re, im], axis=1) / grid_count
+
+        @pl.when(aligned)
+        def _():
+            send(SZ.at[z], SZ.at[z], u_s.at[0], u_r.at[2], dev(x, y, z + 2, c))
+
+        @pl.when(unaligned)
+        def _():
+            for k, dz in enumerate((1, 3)):
+                send(SZ.at[z], SZ.at[z], u_s.at[k], u_r.at[dz], dev(x, y, z + dz, c))
+
+    def project_x():
+        @pl.when(aligned)
+        def _():
+            for dz in (1, 3, 2):
+                arrived(SZ.at[wrap(z - dz)], u_r.at[dz])
+            SO[x] = SZ[0] + SZ[1] + SZ[2] + SZ[3]
+            for e in (1, 3, 2):
+                for cc in range(2):
+                    send(SO.at[x], SO.at[x], w_s.at[e, cc], w_r.at[e], dev(x + e, y, z, cc))
+            send(SO.at[x], SO.at[x], w_s.at[0, 0], w_r.at[0], dev(x, y, z, 1 - c))
+
+    def project_done():
+        @pl.when(unaligned)
+        def _():
+            arrived(SO.at[x], w_r.at[0])
+
+        for e in (1, 3, 2):
+            arrived(SO.at[at(e)], w_r.at[e])
+        for f in range(4):
+            both = SO[f]
+            sub[f, 0] = both[:, 0:64]
+            sub[f, 1] = both[:, 64:128]
+
+    stage("project_z", project_z)
+    stage("image3", image, 3)
+    stage("gathered2", gathered, 2)
+
+    def target(step):
         h = 1 - zh if step < 2 else zh
         cc = 1 - c if step % 2 == 0 else c
-        block = h * 2 + cc
-        total = acc[:, lanes(block)] + image_tile(2, block)
         to_z = h * 2 + c
         dz = wrap(to_z - z)
-        half = total.astype(jnp.bfloat16).reshape(4, 2, 64, 512)
-        if step < 3:
-            SB[step] = half
-            keep(send(SB.at[step], RI.at[dz], i_s.at[step], i_r.at[dz], dev(x, y, to_z, cc)))
-        else:
-            SB[step] = half
-
-            @pl.when(jnp.logical_not(aligned))
-            def _():
-                send(SB.at[3], RI.at[dz], i_s.at[3], i_r.at[dz], dev(x, y, to_z, cc))
-
-            @pl.when(aligned)
-            def _():
+        return h * 2 + cc, cc, to_z, dz, (3 - dz) // 2
+
+    def image_out(step):
+        block, cc, to_z, dz, direct = target(step)
+        total = acc[:, lanes(block)] + image_tile(2, block)
+        half = total.astype(jnp.bfloat16).reshape(2, 2, 2, 64, 512)
+        SB[step] = half
+
+        @pl.when(unaligned)
+        def _():
+            acc[:, lanes(block)] = total
+            send(SB.at[step, direct], RI.at[dz, direct], i_s.at[step, direct], i_r.at[dz, direct], dev(x, y, to_z, cc))
+
+        @pl.when(aligned)
+        def _():
+            if step < 2:
+                send(SB.at[step, 0], RC.at[0, cc], i_s.at[step, 0], k_r.at[0, cc], dev(x, y, z + 1, c))
+                send(SB.at[step, 1], RC.at[1, cc], i_s.at[step, 1], k_r.at[1, cc], dev(x, y, z - 1, c))
+            elif step == 2:
+                send(SB.at[step], RI.at[0], i_s.at[step, 0], i_r.at[0, 0], partner)
+            else:
                 RI[0] = half
 
-    return_sub(
-        mine_sub, sub, SZ, SO, x, y, z, zh, c, aligned, send, keep, arrived, sent, u_s, u_r, w_s, w_r, at
-    )
-
-    for dz in (1, 3, 2):
-        arrived(RI.at[dz], i_r.at[dz])
-
-    @pl.when(jnp.logical_not(aligned))
+    def image_join(step):
+        block, cc, to_z, dz, direct = target(step)
+        joined = 1 - direct
+        arrived(RC.at[joined, cc], k_r.at[joined, cc])
+        rows = pl.ds(pl.multiple_of(joined * 256, 256), 256)
+        total = acc[rows, lanes(block)].reshape(2, 2, 64, 512) + RC[joined, cc].astype(jnp.float32)
+        SB[step, joined] = total.astype(jnp.bfloat16)
+        send(SB.at[step, joined], RI.at[dz, joined], i_s.at[step, joined], i_r.at[dz, joined], dev(x, y, to_z, cc))
+
+    for step in range(4):
+        stage(f"out{step}", image_out, step)
+    stage("project_x", project_x)
+
+    @pl.when(unaligned)
     def _():
-        arrived(RI.at[0], i_r.at[0])
-
-    @pl.loop(0, 4)
-    def _(f):
-        total = RI[0, f].astype(jnp.float32)
-        for dz in (1, 2, 3):
-            total = total + RI[dz, f].astype(jnp.float32)
-        img[f] = total
-
-    for copy in pending:
-        copy.wait_send()
-
-    @pl.when(jnp.logical_not(aligned))
-    def _():
-        sent(xin, v_s.at[0])
-        sent(SB.at[3], i_s.at[3])
-
-
-def return_sub(mine_sub, sub, SZ, SO, x, y, z, zh, c, aligned, send, keep, arrived, sent, u_s, u_r, w_s, w_r, at):
-    SZ[0] = mine_sub
-
-    @pl.when(aligned)
-    def _():
-        SZ[1 + z] = mine_sub
-        send(SZ.at[0], SZ.at[1 + z], u_s.at[0], u_r.at[2], dev(x, y, z + 2, c))
-        for dz in (1, 3, 2):
-            arrived(SZ.at[1 + wrap(z - dz)], u_r.at[dz])
-        SO[x] = SZ[1] + SZ[2] + SZ[3] + SZ[4]
-        for e in (1, 3, 2):
-            for cc in range(2):
-                send(SO.at[x], SO.at[x], w_s.at[e, cc], w_r.at[e], dev(x + e, y, z, cc))
-        send(SO.at[x], SO.at[x], w_s.at[0, 0], w_r.at[0], dev(x, y, z, 1 - c))
-        sent(SZ.at[0], u_s.at[0])
-        for e in (1, 3, 2):
-            for cc in range(2):
-                sent(SO.at[x], w_s.at[e, cc])
-        sent(SO.at[x], w_s.at[0, 0])
-
-    @pl.when(jnp.logical_not(aligned))
-    def _():
-        for k, dz in enumerate((1, 3)):
-            send(SZ.at[0], SZ.at[1 + z], u_s.at[k], u_r.at[dz], dev(x, y, z + dz, c))
-        for k in range(2):
-            sent(SZ.at[0], u_s.at[k])
-        arrived(SO.at[x], w_r.at[0])
-
-    for e in (1, 3, 2):
-        arrived(SO.at[at(e)], w_r.at[e])
-    for f in range(4):
-        both = SO[f]
-        sub[f, 0] = both[:, 0:64]
-        sub[f, 1] = both[:, 64:128]
+        for step in (0, 2, 1, 3):
+            stage(f"join{step}", image_join, step)
+
+    stage("project", project_done)
+
+    def images_done():
+        for dz in (1, 3):
+            for q in range(2):
+                arrived(RI.at[dz, q], i_r.at[dz, q])
+
+        @pl.when(unaligned)
+        def _():
+            arrived(RI.at[0], i_r.at[0, 0])
+
+    stage("images", images_done)
+
+    @pl.loop(0, 2)
+    def _(q):
+        for r in range(2):
+            total = RI[0, q, r].astype(jnp.float32)
+            for dz in (1, 3):
+                total = total + RI[dz, q, r].astype(jnp.float32)
+            img[q * 2 + r] = total
+
+    def drain():
+        for copy in pending:
+            copy.wait_send()
+
+        @pl.when(unaligned)
+        def _():
+            sent(xin, v_s.at[0])
+            for step in range(4):
+                for q in range(2):
+                    sent(SB.at[step, q], i_s.at[step, q])
+            for k in range(2):
+                sent(SZ.at[z], u_s.at[k])
+
+        @pl.when(aligned)
+        def _():
+            for step in range(2):
+                for q in range(2):
+                    sent(SB.at[step, q], i_s.at[step, q])
+            sent(SB.at[2], i_s.at[2, 0])
+            sent(SZ.at[z], u_s.at[0])
+            for e in (1, 3, 2):
+                for cc in range(2):
+                    sent(SO.at[x], w_s.at[e, cc])
+            sent(SO.at[x], w_s.at[0, 0])
+
+    stage("drain", drain)
 
 
 def shards(pair_density, trial_vectors, frequency, val_energy, cond_energy, pair_index):
@@ -387,10 +442,11 @@
             pltpu.VMEM((4, 4, 2, 64, 256), bf),
             pltpu.VMEM((4, 4, 2, 64, 256), bf),
             pltpu.VMEM((4, 2, 64, 512), bf),
-            pltpu.VMEM((4, 4, 2, 64, 512), bf),
-            pltpu.VMEM((4, 4, 2, 64, 512), bf),
+            pltpu.VMEM((4, 2, 2, 2, 64, 512), bf),
+            pltpu.VMEM((4, 2, 2, 2, 64, 512), bf),
+            pltpu.VMEM((2, 2, 2, 2, 64, 512), bf),
             pltpu.VMEM((32, 8, 128), f32),
-            pltpu.VMEM((5, 64, 128), f32),
+            pltpu.VMEM((4, 64, 128), f32),
             pltpu.VMEM((4, 64, 128), f32),
             pltpu.VMEM((256, 128), f32),
             pltpu.VMEM((2, 4, 8, 128), f32),
@@ -401,7 +457,7 @@
             dma((4,)), dma((4, 2)),
             dma((4, 4)), dma((4, 4)),
             dma((4, 4)), dma((4, 4)),
-            dma((4,)), dma((4,)),
+            dma((4, 2)), dma((4, 2)), dma((2, 2)),
             dma, dma,
             dma((2,)), dma((4,)),
             dma((4, 2)), dma((4,)),

time: 122 us -> 99.1 us (0.81); the launches traced: 121 us -> 98.9 us
  Pallas kernels: 114 us -> 92 us
    pallas_call x1, Pallas kernels: 114 us -> 92 us  [shards(): pl.pallas_call(functools.partial(kernel, (prefactor, grid_count)), name='...]
where the time goes in v2:
time: 99.1 us; the launch traced here: 98.9 us
  Pallas kernels  92 us (93%)
  local copies, waits for them, and re-layouts  6.3 us (6%)
    pallas_call x1, Pallas kernels, shards(): pl.pallas_call(functools.partial(kernel, (prefactor, grid_count)), name='...  92 us
    reshape x2, local copies, waits for them, and re-layouts, shards(): pieces = jnp.transpose(pair_density.reshape(32, 2, 4, 2048), (2, 1, 0, 3))  3.29 us
    unnamed x4, local copies, waits for them, and re-layouts  3.01 us

profile of v2, /device:TPU:0, one launch (start us, length us, event | category | flops | bytes accessed | tf_op | source)
XLA Modules:
  0.0 98.9 jit_solution(10349811611151762411)
XLA Ops:
  0.6 1.7 %reshape.8 = bf16[32,2,4,2048]{3,2,1,0:T(4,128)(2,1)S(1)} reshape(bf16[32,2,8192]{2,1,0:T(2,128)(2,1)} %param.6) | data formatting | bytes 2097152 | tf_op jit(solution)/shard_map/reshape | solution.py:422
  2.4 1.5 %copy.13 = bf16[32,2,4,2048]{3,0,1,2:T(8,128)(2,1)} copy(bf16[32,2,4,2048]{3,2,1,0:T(4,128)(2,1)S(1)} %reshape.8) | data formatting | bytes 2097152 | tf_op jit(solution)/shard_map/reshape | solution.py:422
  3.9 92.0 %response.1 = (f32[4,2,64,512]{3,2,1,0:T(8,128)}, f32[4,2,64,64]{3,2,1,0:T(8,128)}) custom-call(bf16[4,2,32,2048]{3,2,1,0:T(8,128)(2,1)} %bitcast.3, bf16[4,2,64,512]{3,2,1,0:T(8,128)(2,1)} %xin.1, s32[32]{0:T(128)} %idx.1, f32[128]{0:T(128)} %cond.1, f32[32]{0:T(128)} %val.1, f32[4]{0:T(128)} %freq.1), custom_call_target="tpu_custom_call" | custom-call | tf_op jit(solution)/shard_map/response/pallas_call | solution.py:427
  95.9 0.0 copy-start
  95.9 2.3 %copy.16 = f32[4,2,64,512]{3,2,1,0:T(8,128)} copy(f32[4,2,64,512]{3,2,1,0:T(8,128)} %get-tuple-element.4) | data formatting | bytes 2097152
  98.2 0.0 copy-done
  98.2 0.7 copy.17
Async XLA Ops:
  95.9 2.3 %copy-start = (f32[4,2,64,64]{3,2,1,0:T(8,128)S(1)}, f32[4,2,64,64]{3,2,1,0:T(8,128)}, u32[]{:S(2)}) copy-start(f32[4,2,64,64]{3,2,1,0:T(8,128)} %get-tuple-element.5) | copy-start | bytes 393220

commit v3 on v2

v3 whole, which is shorter than its diff:
```python
import functools
import math

import jax
import jax.numpy as jnp
from jax import lax
from jax.experimental import pallas as pl
from jax.experimental.pallas import tpu as pltpu
from jax.sharding import PartitionSpec as P

MESH = pl.DeviceIdType.MESH
ORDER = (0, 1, 3, 2)


def wrap(v, n=4):
    return lax.rem(v + n, n)


def dev(x, y, z, c):
    x, y, z, c = wrap(x), wrap(y), wrap(z), wrap(c, 2)
    return (lax.rem(z, 2) * 4 + y, x * 4 + (z // 2) * 2 + c)


def dot_nt(a, b):
    return lax.dot_general(a, b, (((1,), (1,)), ((), ())), preferred_element_type=jnp.float32)


def kernel(
    consts,
    rho, xin, idx, cond, val, freq,
    img, sub,
    R, XF, acc, C32, CB, CR, SF, L, SB, RI, RC, D, SZ, SO, SA, FQ,
    x_s, x_r, y_s, y_r, f_s, f_r, p_s, p_r, v_s, v_r, t_s, c_s, c_r, g_s, g_r,
    i_s, i_r, k_r, d_s, d_r, u_s, u_r, w_s, w_r, q_s, q_r,
):
    prefactor, grid_count = consts
    fi, bi = lax.axis_index("freq"), lax.axis_index("band")
    zl, y = fi // 4, lax.rem(fi, 4)
    x, zh, c = bi // 4, lax.rem(bi // 2, 2), lax.rem(bi, 2)
    z = zh * 2 + zl
    me = (fi, bi)
    partner = dev(x, y, z, 1 - c)
    aligned = zl == c
    unaligned = jnp.logical_not(aligned)
    pending = []

    def send(src, dst, ss, rs, to):
        copy = pltpu.make_async_remote_copy(
            src_ref=src, dst_ref=dst, send_sem=ss, recv_sem=rs, device_id=to, device_id_type=MESH
        )
        copy.start()
        return copy

    def keep(copy):
        pending.append(copy)

    def arrived(dst, rs):
        pltpu.make_async_remote_copy(
            src_ref=dst, dst_ref=dst, send_sem=rs, recv_sem=rs, device_id=me, device_id_type=MESH
        ).wait_recv()

    def sent(src, ss):
        pltpu.make_async_remote_copy(
            src_ref=src, dst_ref=src, send_sem=ss, recv_sem=ss, device_id=me, device_id_type=MESH
        ).wait_send()

    plane = [
        (dy, dx, cc) for dy in range(4) for dx in range(4) for cc in range(2) if (dy, dx, cc) != (0, 0, 0)
    ]
    barrier = pltpu.get_barrier_semaphore()
    for dy, dx, cc in plane:
        pl.semaphore_signal(barrier, inc=1, device_id=dev(x + dx, y + dy, z, c + cc), device_id_type=MESH)
    for dz in (1, 2, 3):
        for cc in range(2):
            pl.semaphore_signal(barrier, inc=1, device_id=dev(x, y, z + dz, cc), device_id_type=MESH)
    with jax.named_scope("entry"):
        pl.semaphore_wait(barrier, len(plane) + 6)

    def lanes(block):
        return pl.ds(pl.multiple_of(block * 512, 512), 512)

    def stage(name, fn, *args):
        with jax.named_scope(name):
            fn(*args)

    def at(e):
        return wrap(x - e)

    def spread(h, e):
        src = rho.at[x, h] if e == 0 else R.at[h, 0, :, at(e), c]
        keep(send(src, R.at[h, 1, :, at(e), c], y_s.at[h, 0, e], y_r.at[h, 0, e], dev(x, y + 1, z, c)))
        keep(send(src, R.at[h, 2, :, at(e), c], y_s.at[h, 1, e], y_r.at[h, 1, e], dev(x, y - 1, z, c)))
        keep(send(src, R.at[h, 0, :, at(e), c], p_s.at[h, 0, e], p_r.at[h, 0, e], partner))

    def pass_on(h, e):
        for side in range(2):
            to = dev(x, y + 1 - 2 * side, z, c)
            piece = R.at[h, 1 + side, :, at(e), c]
            arrived(piece, y_r.at[h, side, e])
            part = R.at[h, 1 + side, side, at(e), c]
            keep(send(part, R.at[h, 3, side, at(e), c], f_s.at[h, side, e], f_r.at[h, side, e], to))
            keep(send(piece, piece, p_s.at[h, 1 + side, e], p_r.at[h, 1 + side, e], partner))

    def pass_far(h, e):
        for side in range(2):
            arrived(R.at[h, 3, side, at(e), c], f_r.at[h, side, e])
        piece = R.at[h, 3, :, at(e), c]
        keep(send(piece, piece, p_s.at[h, 3, e], p_r.at[h, 3, e], partner))

    def partner_done(h, pos):
        for e in ORDER:
            arrived(R.at[h, pos, :, at(e), 1 - c], p_r.at[h, pos, e])

    def from_x(h, e):
        arrived(R.at[h, 0, :, at(e), c], x_r.at[h, e])
        spread(h, e)

    my_lanes = lanes(zh * 2 + c)

    def vector_piece(q, zz, cc):
        return XF.at[pl.ds(2 * q, 2), :, :, lanes((wrap(zz) // 2) * 2 + cc)]

    def begin():
        spread(0, 0)
        for h in range(2):
            for e in (1, 3, 2):
                keep(send(rho.at[wrap(x + e), h], R.at[h, 0, :, x, c], x_s.at[h, e], x_r.at[h, e], dev(x + e, y, z, c)))
        for k in range(2):
            for side in range(2):
                q = (k + side) % 2
                dz = 1 + 2 * side
                keep(send(xin.at[pl.ds(2 * q, 2)], vector_piece(q, z, c), v_s.at[dz, q], v_r.at[dz, c, q], dev(x, y, z + dz, zl)))
        spread(1, 0)

        @pl.when(unaligned)
        def _():
            send(xin, XF.at[:, :, :, my_lanes], v_s.at[0, 0], v_r.at[0, c, 0], partner)

        for f in range(4):
            FQ[0, f] = jnp.full((8, 128), freq[f], jnp.float32)

        lane = lax.broadcasted_iota(jnp.int32, (8, 128), 1)
        row = lax.broadcasted_iota(jnp.int32, (8, 128), 0)
        place = jnp.bitwise_and(row, 1) * 16 + jnp.bitwise_and(lane, 15)
        number = jnp.zeros((8, 128), jnp.int32)
        for i in range(32):
            number = jnp.where(place == i, idx[i], number)
        cond_no = jnp.bitwise_and(number, 127)
        val_no = jnp.right_shift(number, 7)
        zero = jnp.zeros((8, 128), jnp.float32)
        cond_pick = lax.fori_loop(0, 128, lambda j, a: jnp.where(cond_no == j, cond[j], a), zero)
        val_pick = lax.fori_loop(0, 32, lambda j, a: jnp.where(val_no == j, val[j], a), zero)
        D[x * 2 + c] = jnp.where(jnp.right_shift(lane, 4) == x * 2 + c, cond_pick - val_pick, 0.0)
        for h in range(2):
            R[h, 0, :, x, c] = rho[x, h]

        @pl.when(aligned)
        def _():
            XF[:, :, :, my_lanes] = xin[...]
            FQ[1] = FQ[0]

        @pl.when(aligned)
        def _():
            send(FQ.at[0], FQ.at[1], q_s, q_r, dev(x, y, z - 1, c))

        for dy, dx, cc in plane:
            pos = (0, 1, 3, 2)[dy]
            send(D.at[x * 2 + c], D.at[pos * 8 + x * 2 + c], d_s, d_r, dev(x + dx, y + dy, z, c + cc))

    def vectors_pass():
        @pl.when(unaligned)
        def _():
            for q in range(2):
                dz = 1 + 2 * q
                for cc in range(2):
                    piece = vector_piece(q, z - dz, cc)
                    arrived(piece, v_r.at[dz, cc, q])
                    send(piece, piece, t_s.at[q, cc], v_r.at[2, cc, q], dev(x, y, z + dz, c))

    def vectors_done():
        @pl.when(aligned)
        def _():
            arrived(XF.at[:, :, :, lanes(zh * 2 + 1 - c)], v_r.at[0, 1 - c, 0])
            for q in range(2):
                for cc in range(2):
                    arrived(vector_piece(q, z + 2, cc), v_r.at[2, cc, q])

        @pl.when(unaligned)
        def _():
            for q in range(2):
                dz = 3 - 2 * q
                for cc in range(2):
                    arrived(vector_piece(q, z - dz, cc), v_r.at[dz, cc, q])

    A, FAR, B, LAST = (0, 0, 3), (0, 3, 4), (1, 0, 3), (1, 3, 4)

    def cross(h, pos):
        t = dot_nt(XF[...].reshape(512, 2048), R[h, pos].reshape(256, 2048)).reshape(4, 2, 64, 256)
        re = t[:, 0, :, 0:128] + t[:, 1, :, 128:256]
        im = t[:, 1, :, 0:128] - t[:, 0, :, 128:256]
        C32[h, :, pos, 0] = re
        C32[h, :, pos, 1] = im
        CB[h, :, pos, 0] = re.astype(jnp.bfloat16)
        CB[h, :, pos, 1] = im.astype(jnp.bfloat16)

    def cross_out(h, pos):
        for e in (1, 3, 2):
            keep(send(CB.at[h, wrap(x + e), pos], CR.at[h, e, pos], c_s.at[h, pos, e], c_r.at[h, pos, e], dev(x + e, y, z, c)))

    def scale(h, pos):
        for e in (1, 3, 2):
            arrived(CR.at[h, e, pos], c_r.at[h, pos, e])
        own = FQ[1, x][0:1, 0:1]
        total = C32[h, x, pos]
        for e in (1, 2, 3):
            total = total + CR[h, e, pos].astype(jnp.float32)
        delta = D[pos * 8]
        for k in range(1, 8):
            delta = delta + D[pos * 8 + k]
        delta = delta[h : h + 1]
        ratio = delta / (delta * delta + own * own)
        weight = (-4.0 * prefactor * ratio).astype(jnp.bfloat16).astype(jnp.float32)
        SF[h, x, pos] = (weight[None] * total).astype(jnp.bfloat16)
        C32[h, x, pos] = total
        for e in (1, 3, 2):
            keep(send(SF.at[h, x, pos], SF.at[h, x, pos], g_s.at[h, pos, e], g_r.at[h, pos, e], dev(x + e, y, z, c)))

    def project_add(group):
        h = group[0]
        for pos in range(group[1], group[2]):
            flat = C32[h, x, pos].reshape(128, 128)
            high = flat.astype(jnp.bfloat16)
            low = (flat - high.astype(jnp.float32)).astype(jnp.bfloat16)
            part = dot_nt(jnp.concatenate([high, low], axis=0), SF[h, x, pos].reshape(128, 128))
            if h == 0 and pos == 0:
                SA[...] = part
            else:
                SA[...] += part

    def gathered(group):
        h = group[0]
        for pos in range(group[1], group[2]):
            for e in (1, 3, 2):
                arrived(SF.at[h, at(e), pos], g_r.at[h, pos, e])
        for pos in range(group[1], group[2]):
            base = (pos - group[1]) * 256
            re, im = SF[h, :, pos, 0], SF[h, :, pos, 1]
            L[:, 0, :, base : base + 128] = re
            L[:, 0, :, base + 128 : base + 256] = -im
            L[:, 1, :, base : base + 128] = im
            L[:, 1, :, base + 128 : base + 256] = re

    def image_tile(group, block):
        h, some = group[0], pl.ds(group[1], group[2] - group[1])
        depth = (group[2] - group[1]) * 256
        return jnp.dot(
            L[:, :, :, 0:depth].reshape(512, depth),
            R[h, some, :, :, :, :, lanes(block)].reshape(depth, 512),
            preferred_element_type=jnp.float32,
        )

    def image(group):
        gathered(group)
        for block in range(4):
            part = image_tile(group, block)
            if group == A:
                acc[:, block * 512 : block * 512 + 512] = part
            else:
                acc[:, block * 512 : block * 512 + 512] += part

    def energies_done():
        most = D.at[pl.ds(0, 31)]
        arrived(most, d_r)
        sent(most, d_s)

        @pl.when(aligned)
        def _():
            sent(FQ.at[0], q_s)

        @pl.when(unaligned)
        def _():
            arrived(FQ.at[1], q_r)

    stage("begin", begin)
    stage("xA1", from_x, 0, 1)
    stage("xA3", from_x, 0, 3)
    stage("passA0", pass_on, 0, 0)
    stage("xA2", from_x, 0, 2)
    stage("relay", vectors_pass)
    stage("passA1", pass_on, 0, 1)
    stage("passA3", pass_on, 0, 3)
    stage("xB1", from_x, 1, 1)
    stage("xB3", from_x, 1, 3)
    stage("farA0", pass_far, 0, 0)
    stage("passA2", pass_on, 0, 2)
    stage("passB0", pass_on, 1, 0)
    stage("xB2", from_x, 1, 2)
    stage("vectors", vectors_done)
    stage("partA0", partner_done, 0, 0)
    stage("crossA0", cross, 0, 0)
    stage("outA0", cross_out, 0, 0)
    stage("farA1", pass_far, 0, 1)
    stage("partA1", partner_done, 0, 1)
    stage("crossA1", cross, 0, 1)
    stage("outA1", cross_out, 0, 1)
    stage("farA3", pass_far, 0, 3)
    stage("partA2", partner_done, 0, 2)
    stage("crossA2", cross, 0, 2)
    stage("outA2", cross_out, 0, 2)
    stage("partB0", partner_done, 1, 0)
    stage("crossB0", cross, 1, 0)
    stage("outB0", cross_out, 1, 0)
    stage("passB1", pass_on, 1, 1)
    stage("energies", energies_done)
    stage("scaleA0", scale, 0, 0)
    stage("scaleA1", scale, 0, 1)
    stage("passB3", pass_on, 1, 3)
    stage("farA2", pass_far, 0, 2)
    stage("partA3", partner_done, 0, 3)
    stage("crossA3", cross, 0, 3)
    stage("outA3", cross_out, 0, 3)
    stage("scaleA2", scale, 0, 2)
    stage("passB2", pass_on, 1, 2)
    stage("farB0", pass_far, 1, 0)
    stage("partB1", partner_done, 1, 1)
    stage("crossB1", cross, 1, 1)
    stage("outB1", cross_out, 1, 1)
    stage("scaleB0", scale, 1, 0)
    stage("farB1", pass_far, 1, 1)
    stage("partB2", partner_done, 1, 2)
    stage("crossB2", cross, 1, 2)
    stage("outB2", cross_out, 1, 2)
    stage("farB3", pass_far, 1, 3)
    stage("scaleA3", scale, 0, 3)
    stage("farB2", pass_far, 1, 2)
    stage("partB3", partner_done, 1, 3)
    stage("crossB3", cross, 1, 3)
    stage("outB3", cross_out, 1, 3)
    stage("scaleB1", scale, 1, 1)
    stage("imageA", image, A)
    stage("scaleB2", scale, 1, 2)
    stage("scaleB3", scale, 1, 3)
    stage("imageF", image, FAR)
    stage("addA", project_add, A)
    stage("addF", project_add, FAR)
    stage("addB", project_add, B)
    stage("addL", project_add, LAST)

    def project_z():
        both = SA[0:128] + SA[128:256]
        re = both[0:64, 0:64] + both[64:128, 64:128]
        im = both[0:64, 64:128] - both[64:128, 0:64]
        SZ[z] = jnp.concatenate([re, im], axis=1) / grid_count

        @pl.when(aligned)
        def _():
            send(SZ.at[z], SZ.at[z], u_s.at[0], u_r.at[2], dev(x, y, z + 2, c))

        @pl.when(unaligned)
        def _():
            for k, dz in enumerate((1, 3)):
                send(SZ.at[z], SZ.at[z], u_s.at[k], u_r.at[dz], dev(x, y, z + dz, c))

    def project_x():
        @pl.when(aligned)
        def _():
            for dz in (1, 3, 2):
                arrived(SZ.at[wrap(z - dz)], u_r.at[dz])
            SO[x] = SZ[0] + SZ[1] + SZ[2] + SZ[3]
            for e in (1, 3, 2):
                for cc in range(2):
                    send(SO.at[x], SO.at[x], w_s.at[e, cc], w_r.at[e], dev(x + e, y, z, cc))
            send(SO.at[x], SO.at[x], w_s.at[0, 0], w_r.at[0], dev(x, y, z, 1 - c))

    def project_done():
        @pl.when(unaligned)
        def _():
            arrived(SO.at[x], w_r.at[0])

        for e in (1, 3, 2):
            arrived(SO.at[at(e)], w_r.at[e])
        for f in range(4):
            both = SO[f]
            sub[f, 0] = both[:, 0:64]
            sub[f, 1] = both[:, 64:128]

    stage("project_z", project_z)
    stage("imageB", image, B)
    stage("gatheredL", gathered, LAST)

    def target(step):
        h = 1 - zh if step < 2 else zh
        cc = 1 - c if step % 2 == 0 else c
        to_z = h * 2 + c
        dz = wrap(to_z - z)
        return h * 2 + cc, cc, to_z, dz, (3 - dz) // 2

    def image_out(step):
        block, cc, to_z, dz, direct = target(step)
        total = acc[:, lanes(block)] + image_tile(LAST, block)
        half = total.astype(jnp.bfloat16).reshape(2, 2, 2, 64, 512)
        SB[step] = half

        @pl.when(unaligned)
        def _():
            acc[:, lanes(block)] = total
            send(SB.at[step, direct], RI.at[dz, direct], i_s.at[step, direct], i_r.at[dz, direct], dev(x, y, to_z, cc))

        @pl.when(aligned)
        def _():
            if step < 2:
                send(SB.at[step, 0], RC.at[0, cc], i_s.at[step, 0], k_r.at[0, cc], dev(x, y, z + 1, c))
                send(SB.at[step, 1], RC.at[1, cc], i_s.at[step, 1], k_r.at[1, cc], dev(x, y, z - 1, c))
            elif step == 2:
                send(SB.at[step], RI.at[0], i_s.at[step, 0], i_r.at[0, 0], partner)
            else:
                RI[0] = half

    def image_join(step):
        block, cc, to_z, dz, direct = target(step)
        joined = 1 - direct
        arrived(RC.at[joined, cc], k_r.at[joined, cc])
        rows = pl.ds(pl.multiple_of(joined * 256, 256), 256)
        total = acc[rows, lanes(block)].reshape(2, 2, 64, 512) + RC[joined, cc].astype(jnp.float32)
        SB[step, joined] = total.astype(jnp.bfloat16)
        send(SB.at[step, joined], RI.at[dz, joined], i_s.at[step, joined], i_r.at[dz, joined], dev(x, y, to_z, cc))

    for step in range(4):
        stage(f"out{step}", image_out, step)
    stage("project_x", project_x)

    @pl.when(unaligned)
    def _():
        for step in (0, 2, 1, 3):
            stage(f"join{step}", image_join, step)

    stage("project", project_done)

    def images_done():
        for dz in (1, 3):
            for q in range(2):
                arrived(RI.at[dz, q], i_r.at[dz, q])

        @pl.when(unaligned)
        def _():
            arrived(RI.at[0], i_r.at[0, 0])

    stage("images", images_done)

    @pl.loop(0, 2)
    def _(q):
        for r in range(2):
            total = RI[0, q, r].astype(jnp.float32)
            for dz in (1, 3):
                total = total + RI[dz, q, r].astype(jnp.float32)
            img[q * 2 + r] = total

    def drain():
        for copy in pending:
            copy.wait_send()

        @pl.when(unaligned)
        def _():
            sent(xin, v_s.at[0, 0])
            for q in range(2):
                for cc in range(2):
                    sent(vector_piece(q, z - 1 - 2 * q, cc), t_s.at[q, cc])
            for step in range(4):
                for q in range(2):
                    sent(SB.at[step, q], i_s.at[step, q])
            for k in range(2):
                sent(SZ.at[z], u_s.at[k])

        @pl.when(aligned)
        def _():
            for step in range(2):
                for q in range(2):
                    sent(SB.at[step, q], i_s.at[step, q])
            sent(SB.at[2], i_s.at[2, 0])
            sent(SZ.at[z], u_s.at[0])
            for e in (1, 3, 2):
                for cc in range(2):
                    sent(SO.at[x], w_s.at[e, cc])
            sent(SO.at[x], w_s.at[0, 0])

    stage("drain", drain)


def shards(pair_density, trial_vectors, frequency, val_energy, cond_energy, pair_index):
    groups = lax.axis_size("freq")
    members = lax.axis_size("band")
    pair_count = pair_density.shape[0] * groups * members
    grid_count = trial_vectors.shape[3] * members
    prefactor = 1.0 / math.sqrt(2.0 * grid_count * pair_count)
    pieces = jnp.transpose(pair_density.reshape(2, 16, 2, 4, 2048), (3, 0, 2, 1, 4))
    bf, f32 = jnp.bfloat16, jnp.float32
    vmem = pl.BlockSpec(memory_space=pltpu.VMEM)
    smem = pl.BlockSpec(memory_space=pltpu.SMEM)
    dma = pltpu.SemaphoreType.DMA
    return pl.pallas_call(
        functools.partial(kernel, (prefactor, grid_count)),
        name="response",
        out_shape=(
            jax.ShapeDtypeStruct((4, 2, 64, 512), f32),
            jax.ShapeDtypeStruct((4, 2, 64, 64), f32),
        ),
        in_specs=[vmem, vmem, smem, smem, smem, smem],
        out_specs=(vmem, vmem),
        scratch_shapes=[
            pltpu.VMEM((2, 4, 2, 4, 2, 16, 2048), bf),
            pltpu.VMEM((4, 2, 64, 2048), bf),
            pltpu.VMEM((512, 2048), f32),
            pltpu.VMEM((2, 4, 4, 2, 64, 128), f32),
            pltpu.VMEM((2, 4, 4, 2, 64, 128), bf),
            pltpu.VMEM((2, 4, 4, 2, 64, 128), bf),
            pltpu.VMEM((2, 4, 4, 2, 64, 128), bf),
            pltpu.VMEM((4, 2, 64, 768), bf),
            pltpu.VMEM((4, 2, 2, 2, 64, 512), bf),
            pltpu.VMEM((4, 2, 2, 2, 64, 512), bf),
            pltpu.VMEM((2, 2, 2, 2, 64, 512), bf),
            pltpu.VMEM((32, 8, 128), f32),
            pltpu.VMEM((4, 64, 128), f32),
            pltpu.VMEM((4, 64, 128), f32),
            pltpu.VMEM((256, 128), f32),
            pltpu.VMEM((2, 4, 8, 128), f32),
            dma((2, 4)), dma((2, 4)),
            dma((2, 2, 4)), dma((2, 2, 4)),
            dma((2, 2, 4)), dma((2, 2, 4)),
            dma((2, 4, 4)), dma((2, 4, 4)),
            dma((4, 2)), dma((4, 2, 2)), dma((2, 2)),
            dma((2, 4, 4)), dma((2, 4, 4)),
            dma((2, 4, 4)), dma((2, 4, 4)),
            dma((4, 2)), dma((4, 2)), dma((2, 2)),
            dma, dma,
            dma((2,)), dma((4,)),
            dma((4, 2)), dma((4,)),
            dma, dma,
        ],
        compiler_params=pltpu.CompilerParams(
            collective_id=0, has_side_effects=True, vmem_limit_bytes=56 * 2**20
        ),
    )(pieces, trial_vectors, pair_index, cond_energy, val_energy, frequency)


def solution(mesh):
    return jax.shard_map(
        shards,
        mesh=mesh,
        in_specs=(
            P(("freq", "band"), None, None),
            P("freq", None, None, "band"),
            P("freq"),
            P(),
            P(),
            P(("freq", "band")),
        ),
        out_specs=(P("freq", None, None, "band"), P("freq", None, None, None)),
        check_vma=False,
    )
```

time: 99.1 us -> 91.8 us (0.926)
  Pallas kernels: 92 us -> 84.7 us
    pallas_call x1, Pallas kernels: 92 us -> 84.7 us  [shards(): pl.pallas_call(functools.partial(kernel, (prefactor, grid_count)), name='...]
where the time goes in v3:
time: 91.8 us; the launch traced here: 91.6 us
  Pallas kernels  84.7 us (92%)
  local copies, waits for them, and re-layouts  6.3 us (7%)
    pallas_call x1, Pallas kernels, shards(): pl.pallas_call(functools.partial(kernel, (prefactor, grid_count)), name='...  84.7 us
    reshape x2, local copies, waits for them, and re-layouts, shards(): pair_density.reshape(2, 16, 2, 4, 2048)  3.29 us
    unnamed x4, local copies, waits for them, and re-layouts  3.01 us

profile of v3, /device:TPU:0, one launch (start us, length us, event | category | flops | bytes accessed | tf_op | source)
XLA Modules:
  0.0 91.6 jit_solution(12413027930561335351)
XLA Ops:
  0.6 1.7 %reshape.8 = bf16[2,16,2,4,2048]{4,3,2,1,0:T(4,128)(2,1)S(1)} reshape(bf16[32,2,8192]{2,1,0:T(2,128)(2,1)} %param.6) | data formatting | bytes 2097152 | tf_op jit(solution)/shard_map/reshape | solution.py:495
  2.4 1.5 %copy.13 = bf16[2,16,2,4,2048]{4,1,2,0,3:T(8,128)(2,1)} copy(bf16[2,16,2,4,2048]{4,3,2,1,0:T(4,128)(2,1)S(1)} %reshape.8) | data formatting | bytes 2097152 | tf_op jit(solution)/shard_map/reshape | solution.py:495
  3.9 84.7 %response.1 = (f32[4,2,64,512]{3,2,1,0:T(8,128)}, f32[4,2,64,64]{3,2,1,0:T(8,128)}) custom-call(bf16[4,2,2,16,2048]{4,3,2,1,0:T(8,128)(2,1)} %bitcast.3, bf16[4,2,64,512]{3,2,1,0:T(8,128)(2,1)} %xin.1, s32[32]{0:T(128)} %idx.1, f32[128]{0:T(128)} %cond.1, f32[32]{0:T(128)} %val.1, f32[4]{0:T(128)} %freq.1), custom_call_target="tpu_custom_call" | custom-call | tf_op jit(solution)/shard_map/response/pallas_call | solution.py:500
  88.6 0.0 copy-start
  88.6 2.3 %copy.16 = f32[4,2,64,512]{3,2,1,0:T(8,128)} copy(f32[4,2,64,512]{3,2,1,0:T(8,128)} %get-tuple-element.4) | data formatting | bytes 2097152
  90.9 0.0 copy-done
  90.9 0.7 copy.17
Async XLA Ops:
  88.6 2.3 %copy-start = (f32[4,2,64,64]{3,2,1,0:T(8,128)S(1)}, f32[4,2,64,64]{3,2,1,0:T(8,128)}, u32[]{:S(2)}) copy-start(f32[4,2,64,64]{3,2,1,0:T(8,128)} %get-tuple-element.5) | copy-start | bytes 393220

commit v4 on v3

--- a/solution.py
+++ b/solution.py
@@ -28,8 +28,8 @@
 def kernel(
     consts,
     rho, xin, idx, cond, val, freq,
-    img, sub,
-    R, XF, acc, C32, CB, CR, SF, L, SB, RI, RC, D, SZ, SO, SA, FQ,
+    RI, sub,
+    R, XF, acc, C32, CB, CR, SF, L, SB, RC, D, SZ, SO, SA, FQ,
     x_s, x_r, y_s, y_r, f_s, f_r, p_s, p_r, v_s, v_r, t_s, c_s, c_r, g_s, g_r,
     i_s, i_r, k_r, d_s, d_r, u_s, u_r, w_s, w_r, q_s, q_r,
 ):
@@ -86,8 +86,14 @@
     def at(e):
         return wrap(x - e)
 
+    def columns(block):
+        return pl.ds(pl.multiple_of(block * 2048, 2048), 2048)
+
+    def own_piece(h, block):
+        return rho.at[:, pl.ds(16 * h, 16), columns(block)]
+
     def spread(h, e):
-        src = rho.at[x, h] if e == 0 else R.at[h, 0, :, at(e), c]
+        src = own_piece(h, x) if e == 0 else R.at[h, 0, :, at(e), c]
         keep(send(src, R.at[h, 1, :, at(e), c], y_s.at[h, 0, e], y_r.at[h, 0, e], dev(x, y + 1, z, c)))
         keep(send(src, R.at[h, 2, :, at(e), c], y_s.at[h, 1, e], y_r.at[h, 1, e], dev(x, y - 1, z, c)))
         keep(send(src, R.at[h, 0, :, at(e), c], p_s.at[h, 0, e], p_r.at[h, 0, e], partner))
@@ -124,7 +130,7 @@
         spread(0, 0)
         for h in range(2):
             for e in (1, 3, 2):
-                keep(send(rho.at[wrap(x + e), h], R.at[h, 0, :, x, c], x_s.at[h, e], x_r.at[h, e], dev(x + e, y, z, c)))
+                keep(send(own_piece(h, wrap(x + e)), R.at[h, 0, :, x, c], x_s.at[h, e], x_r.at[h, e], dev(x + e, y, z, c)))
         for k in range(2):
             for side in range(2):
                 q = (k + side) % 2
@@ -152,7 +158,7 @@
         val_pick = lax.fori_loop(0, 32, lambda j, a: jnp.where(val_no == j, val[j], a), zero)
         D[x * 2 + c] = jnp.where(jnp.right_shift(lane, 4) == x * 2 + c, cond_pick - val_pick, 0.0)
         for h in range(2):
-            R[h, 0, :, x, c] = rho[x, h]
+            R[h, 0, :, x, c] = rho[:, 16 * h : 16 * h + 16, columns(x)]
 
         @pl.when(aligned)
         def _():
@@ -393,10 +399,10 @@
         cc = 1 - c if step % 2 == 0 else c
         to_z = h * 2 + c
         dz = wrap(to_z - z)
-        return h * 2 + cc, cc, to_z, dz, (3 - dz) // 2
+        return h * 2 + cc, cc, to_z, (dz + 1) // 2, (3 - dz) // 2
 
     def image_out(step):
-        block, cc, to_z, dz, direct = target(step)
+        block, cc, to_z, slot, direct = target(step)
         total = acc[:, lanes(block)] + image_tile(LAST, block)
         half = total.astype(jnp.bfloat16).reshape(2, 2, 2, 64, 512)
         SB[step] = half
@@ -404,7 +410,7 @@
         @pl.when(unaligned)
         def _():
             acc[:, lanes(block)] = total
-            send(SB.at[step, direct], RI.at[dz, direct], i_s.at[step, direct], i_r.at[dz, direct], dev(x, y, to_z, cc))
+            send(SB.at[step, direct], RI.at[slot, direct], i_s.at[step, direct], i_r.at[slot, direct], dev(x, y, to_z, cc))
 
         @pl.when(aligned)
         def _():
@@ -417,13 +423,13 @@
                 RI[0] = half
 
     def image_join(step):
-        block, cc, to_z, dz, direct = target(step)
+        block, cc, to_z, slot, direct = target(step)
         joined = 1 - direct
         arrived(RC.at[joined, cc], k_r.at[joined, cc])
         rows = pl.ds(pl.multiple_of(joined * 256, 256), 256)
         total = acc[rows, lanes(block)].reshape(2, 2, 64, 512) + RC[joined, cc].astype(jnp.float32)
         SB[step, joined] = total.astype(jnp.bfloat16)
-        send(SB.at[step, joined], RI.at[dz, joined], i_s.at[step, joined], i_r.at[dz, joined], dev(x, y, to_z, cc))
+        send(SB.at[step, joined], RI.at[slot, joined], i_s.at[step, joined], i_r.at[slot, joined], dev(x, y, to_z, cc))
 
     for step in range(4):
         stage(f"out{step}", image_out, step)
@@ -437,23 +443,15 @@
     stage("project", project_done)
 
     def images_done():
-        for dz in (1, 3):
+        for slot in (1, 2):
             for q in range(2):
-                arrived(RI.at[dz, q], i_r.at[dz, q])
+                arrived(RI.at[slot, q], i_r.at[slot, q])
 
         @pl.when(unaligned)
         def _():
             arrived(RI.at[0], i_r.at[0, 0])
 
     stage("images", images_done)
-
-    @pl.loop(0, 2)
-    def _(q):
-        for r in range(2):
-            total = RI[0, q, r].astype(jnp.float32)
-            for dz in (1, 3):
-                total = total + RI[dz, q, r].astype(jnp.float32)
-            img[q * 2 + r] = total
 
     def drain():
         for copy in pending:
@@ -492,16 +490,16 @@
     pair_count = pair_density.shape[0] * groups * members
     grid_count = trial_vectors.shape[3] * members
     prefactor = 1.0 / math.sqrt(2.0 * grid_count * pair_count)
-    pieces = jnp.transpose(pair_density.reshape(2, 16, 2, 4, 2048), (3, 0, 2, 1, 4))
+    pieces = jnp.transpose(pair_density, (1, 0, 2))
     bf, f32 = jnp.bfloat16, jnp.float32
     vmem = pl.BlockSpec(memory_space=pltpu.VMEM)
     smem = pl.BlockSpec(memory_space=pltpu.SMEM)
     dma = pltpu.SemaphoreType.DMA
-    return pl.pallas_call(
+    parts, subspace = pl.pallas_call(
         functools.partial(kernel, (prefactor, grid_count)),
         name="response",
         out_shape=(
-            jax.ShapeDtypeStruct((4, 2, 64, 512), f32),
+            jax.ShapeDtypeStruct((3, 2, 2, 2, 64, 512), bf),
             jax.ShapeDtypeStruct((4, 2, 64, 64), f32),
         ),
         in_specs=[vmem, vmem, smem, smem, smem, smem],
@@ -515,7 +513,6 @@
             pltpu.VMEM((2, 4, 4, 2, 64, 128), bf),
             pltpu.VMEM((2, 4, 4, 2, 64, 128), bf),
             pltpu.VMEM((4, 2, 64, 768), bf),
-            pltpu.VMEM((4, 2, 2, 2, 64, 512), bf),
             pltpu.VMEM((4, 2, 2, 2, 64, 512), bf),
             pltpu.VMEM((2, 2, 2, 2, 64, 512), bf),
             pltpu.VMEM((32, 8, 128), f32),
@@ -537,9 +534,11 @@
             dma, dma,
         ],
         compiler_params=pltpu.CompilerParams(
-            collective_id=0, has_side_effects=True, vmem_limit_bytes=56 * 2**20
+            collective_id=0, has_side_effects=True, vmem_limit_bytes=36 * 2**20
         ),
     )(pieces, trial_vectors, pair_index, cond_energy, val_energy, frequency)
+    images = parts[0].astype(f32) + parts[1].astype(f32) + parts[2].astype(f32)
+    return images.reshape(4, 2, 64, 512), subspace
 
 
 def solution(mesh):

time: 91.8 us -> 87.3 us (0.951)
  local copies, waits for them, and re-layouts: 6.3 us -> 2.59 us
  Pallas kernels: 84.7 us -> 82.7 us
  other arithmetic: 0 us -> 1.18 us
    reshape x2 -> x0, local copies, waits for them, and re-layouts: 3.29 us -> none  [shards(): pair_density.reshape(2, 16, 2, 4, 2048)]
    pallas_call x1, Pallas kernels: 84.7 us -> 82.7 us  [shards(): pl.pallas_call(functools.partial(kernel, (prefactor, grid_count)), name='...]
    add x0 -> x1, other arithmetic: none -> 1.18 us  [shards(): images = parts[0].astype(f32) + parts[1].astype(f32) + parts[2].astype(f32)]
    unnamed x4 -> x12, local copies, waits for them, and re-layouts: 3.01 us -> 2.59 us
where the time goes in v4:
time: 87.3 us; the launch traced here: 87.2 us
  Pallas kernels  82.7 us (95%)
  local copies, waits for them, and re-layouts  2.59 us (3%)
  other arithmetic  1.18 us (1%)
    pallas_call x1, Pallas kernels, shards(): pl.pallas_call(functools.partial(kernel, (prefactor, grid_count)), name='...  82.7 us
    unnamed x12, local copies, waits for them, and re-layouts  2.59 us

profile of v4, /device:TPU:0, one launch (start us, length us, event | category | flops | bytes accessed | tf_op | source)
XLA Modules:
  0.0 87.2 jit_solution(15821640071886782961)
XLA Ops:
  0.6 0.0 copy-start.1
  0.6 0.0 copy-start.2
  0.7 0.0 copy-start.3
  0.7 0.0 copy-start.4
  0.7 0.0 copy-start
  0.7 1.9 %copy.10 = bf16[32,2,8192]{2,0,1:T(8,128)(2,1)S(1)} copy(bf16[32,2,8192]{2,1,0:T(2,128)(2,1)} %param.6) | data formatting | bytes 2097152 | tf_op args[0]
  2.5 0.0 copy-done.1
  2.6 0.0 copy-done.2
  2.6 0.0 copy-done.3
  2.6 0.0 copy-done.4
  2.6 0.0 copy-done
  2.6 82.7 %response.1 = (bf16[3,2,2,2,64,512]{5,4,3,2,1,0:T(8,128)(2,1)S(1)}, f32[4,2,64,64]{3,2,1,0:T(8,128)S(1)}) custom-call(bf16[2,32,8192]{2,1,0:T(8,128)(2,1)S(1)} %bitcast.4, bf16[4,2,64,512]{3,2,1,0:T(8,128)(2,1)S(1)} %copy-done, s32[32]{0:T(128)S(1)} %copy-done.1, f32[128]{0:T(128)S(1)} %copy-done.2, f32[32]{0:T(128)S(1)} %copy-done.3, f32[4]{0:T(128)S(1)} %copy-done.4), custom_call_target="tpu_custom_call" | custom-call | tf_op jit(solution)/shard_map/response/pallas_call | solution.py:498
  85.3 1.2 %convert_add_fusion = f32[1,2,2,2,64,512]{5,4,3,2,1,0:T(8,128)} fusion(bf16[3,2,2,2,64,512]{5,4,3,2,1,0:T(8,128)(2,1)S(1)} %get-tuple-element.4), kind=kLoop, calls=%fused_computation.1 | loop fusion | flops 1310720 | bytes 2621440 | tf_op jit(solution)/shard_map/add | solution.py:540
  86.5 0.7 copy.12
Async XLA Ops:
  0.6 1.9 %copy-start.1 = (s32[32]{0:T(128)S(1)}, s32[32]{0:T(128)}, u32[]{:S(2)}) copy-start(s32[32]{0:T(128)} %idx.1) | copy-start | bytes 388
  0.6 1.9 %copy-start.2 = (f32[128]{0:T(128)S(1)}, f32[128]{0:T(128)}, u32[]{:S(2)}) copy-start(f32[128]{0:T(128)} %cond.1) | copy-start | bytes 1540
  0.7 1.9 %copy-start.3 = (f32[32]{0:T(128)S(1)}, f32[32]{0:T(128)}, u32[]{:S(2)}) copy-start(f32[32]{0:T(128)} %val.1) | copy-start | bytes 388
  0.7 1.9 %copy-start.4 = (f32[4]{0:T(128)S(1)}, f32[4]{0:T(128)}, u32[]{:S(2)}) copy-start(f32[4]{0:T(128)} %freq.1) | copy-start | bytes 52
  0.7 1.9 %copy-start = (bf16[4,2,64,512]{3,2,1,0:T(8,128)(2,1)S(1)}, bf16[4,2,64,512]{3,2,1,0:T(8,128)(2,1)}, u32[]{:S(2)}) copy-start(bf16[4,2,64,512]{3,2,1,0:T(8,128)(2,1)} %xin.1) | copy-start | bytes 1572868

commit v5 on v4

--- a/solution.py
+++ b/solution.py
@@ -198,7 +198,7 @@
                 for cc in range(2):
                     arrived(vector_piece(q, z - dz, cc), v_r.at[dz, cc, q])
 
-    A, FAR, B, LAST = (0, 0, 3), (0, 3, 4), (1, 0, 3), (1, 3, 4)
+    A, FAR, B, LAST = (0, 0, 3), (0, 3, 4), (1, 0, 2), (1, 2, 4)
 
     def cross(h, pos):
         t = dot_nt(XF[...].reshape(512, 2048), R[h, pos].reshape(256, 2048)).reshape(4, 2, 64, 256)
@@ -210,7 +210,7 @@
         CB[h, :, pos, 1] = im.astype(jnp.bfloat16)
 
     def cross_out(h, pos):
-        for e in (1, 3, 2):
+        for e in (2, 1, 3):
             keep(send(CB.at[h, wrap(x + e), pos], CR.at[h, e, pos], c_s.at[h, pos, e], c_r.at[h, pos, e], dev(x + e, y, z, c)))
 
     def scale(h, pos):
@@ -228,7 +228,7 @@
         weight = (-4.0 * prefactor * ratio).astype(jnp.bfloat16).astype(jnp.float32)
         SF[h, x, pos] = (weight[None] * total).astype(jnp.bfloat16)
         C32[h, x, pos] = total
-        for e in (1, 3, 2):
+        for e in (2, 1, 3):
             keep(send(SF.at[h, x, pos], SF.at[h, x, pos], g_s.at[h, pos, e], g_r.at[h, pos, e], dev(x + e, y, z, c)))
 
     def project_add(group):
@@ -326,19 +326,19 @@
     stage("crossA3", cross, 0, 3)
     stage("outA3", cross_out, 0, 3)
     stage("scaleA2", scale, 0, 2)
+    stage("scaleB0", scale, 1, 0)
     stage("passB2", pass_on, 1, 2)
     stage("farB0", pass_far, 1, 0)
     stage("partB1", partner_done, 1, 1)
     stage("crossB1", cross, 1, 1)
     stage("outB1", cross_out, 1, 1)
-    stage("scaleB0", scale, 1, 0)
     stage("farB1", pass_far, 1, 1)
+    stage("farB3", pass_far, 1, 3)
+    stage("farB2", pass_far, 1, 2)
+    stage("scaleA3", scale, 0, 3)
     stage("partB2", partner_done, 1, 2)
     stage("crossB2", cross, 1, 2)
     stage("outB2", cross_out, 1, 2)
-    stage("farB3", pass_far, 1, 3)
-    stage("scaleA3", scale, 0, 3)
-    stage("farB2", pass_far, 1, 2)
     stage("partB3", partner_done, 1, 3)
     stage("crossB3", cross, 1, 3)
     stage("outB3", cross_out, 1, 3)

time: 87.3 us -> 85.6 us (0.981)
  Pallas kernels: 82.7 us -> 80.9 us
    pallas_call x1, Pallas kernels: 82.7 us -> 80.9 us  [shards(): pl.pallas_call(functools.partial(kernel, (prefactor, grid_count)), name='...]
where the time goes in v5:
time: 85.6 us; the launch traced here: 85.4 us
  Pallas kernels  80.9 us (95%)
  local copies, waits for them, and re-layouts  2.59 us (3%)
  other arithmetic  1.18 us (1%)
    pallas_call x1, Pallas kernels, shards(): pl.pallas_call(functools.partial(kernel, (prefactor, grid_count)), name='...  80.9 us
    unnamed x12, local copies, waits for them, and re-layouts  2.59 us

profile of v5, /device:TPU:0, one launch (start us, length us, event | category | flops | bytes accessed | tf_op | source)
XLA Modules:
  0.0 85.4 jit_solution(11021199040960773945)
XLA Ops:
  0.6 0.0 copy-start.1
  0.6 0.0 copy-start.2
  0.7 0.0 copy-start.3
  0.7 0.0 copy-start.4
  0.7 0.0 copy-start
  0.7 1.9 %copy.10 = bf16[32,2,8192]{2,0,1:T(8,128)(2,1)S(1)} copy(bf16[32,2,8192]{2,1,0:T(2,128)(2,1)} %param.6) | data formatting | bytes 2097152 | tf_op args[0]
  2.5 0.0 copy-done.1
  2.6 0.0 copy-done.2
  2.6 0.0 copy-done.3
  2.6 0.0 copy-done.4
  2.6 0.0 copy-done
  2.6 80.9 %response.1 = (bf16[3,2,2,2,64,512]{5,4,3,2,1,0:T(8,128)(2,1)S(1)}, f32[4,2,64,64]{3,2,1,0:T(8,128)S(1)}) custom-call(bf16[2,32,8192]{2,1,0:T(8,128)(2,1)S(1)} %bitcast.4, bf16[4,2,64,512]{3,2,1,0:T(8,128)(2,1)S(1)} %copy-done, s32[32]{0:T(128)S(1)} %copy-done.1, f32[128]{0:T(128)S(1)} %copy-done.2, f32[32]{0:T(128)S(1)} %copy-done.3, f32[4]{0:T(128)S(1)} %copy-done.4), custom_call_target="tpu_custom_call" | custom-call | tf_op jit(solution)/shard_map/response/pallas_call | solution.py:498
  83.6 1.2 %convert_add_fusion = f32[1,2,2,2,64,512]{5,4,3,2,1,0:T(8,128)} fusion(bf16[3,2,2,2,64,512]{5,4,3,2,1,0:T(8,128)(2,1)S(1)} %get-tuple-element.4), kind=kLoop, calls=%fused_computation.1 | loop fusion | flops 1310720 | bytes 2621440 | tf_op jit(solution)/shard_map/add | solution.py:540
  84.7 0.7 copy.12
Async XLA Ops:
  0.6 1.9 %copy-start.1 = (s32[32]{0:T(128)S(1)}, s32[32]{0:T(128)}, u32[]{:S(2)}) copy-start(s32[32]{0:T(128)} %idx.1) | copy-start | bytes 388
  0.6 1.9 %copy-start.2 = (f32[128]{0:T(128)S(1)}, f32[128]{0:T(128)}, u32[]{:S(2)}) copy-start(f32[128]{0:T(128)} %cond.1) | copy-start | bytes 1540
  0.7 1.9 %copy-start.3 = (f32[32]{0:T(128)S(1)}, f32[32]{0:T(128)}, u32[]{:S(2)}) copy-start(f32[32]{0:T(128)} %val.1) | copy-start | bytes 388
  0.7 1.9 %copy-start.4 = (f32[4]{0:T(128)S(1)}, f32[4]{0:T(128)}, u32[]{:S(2)}) copy-start(f32[4]{0:T(128)} %freq.1) | copy-start | bytes 52
  0.7 1.9 %copy-start = (bf16[4,2,64,512]{3,2,1,0:T(8,128)(2,1)S(1)}, bf16[4,2,64,512]{3,2,1,0:T(8,128)(2,1)}, u32[]{:S(2)}) copy-start(bf16[4,2,64,512]{3,2,1,0:T(8,128)(2,1)} %xin.1) | copy-start | bytes 1572868

commit v6 on v5

--- a/solution.py
+++ b/solution.py
@@ -64,17 +64,15 @@
             src_ref=src, dst_ref=src, send_sem=ss, recv_sem=ss, device_id=me, device_id_type=MESH
         ).wait_send()
 
-    plane = [
-        (dy, dx, cc) for dy in range(4) for dx in range(4) for cc in range(2) if (dy, dx, cc) != (0, 0, 0)
-    ]
+    lines = [dev(x + e, y, z, cc) for e in (1, 2, 3) for cc in range(2)]
+    lines += [dev(x, y + dy, z, c) for dy in (1, 2, 3)]
+    lines += [dev(x, y, z + dz, cc) for dz in (1, 2, 3) for cc in range(2)]
+    lines.append(partner)
     barrier = pltpu.get_barrier_semaphore()
-    for dy, dx, cc in plane:
-        pl.semaphore_signal(barrier, inc=1, device_id=dev(x + dx, y + dy, z, c + cc), device_id_type=MESH)
-    for dz in (1, 2, 3):
-        for cc in range(2):
-            pl.semaphore_signal(barrier, inc=1, device_id=dev(x, y, z + dz, cc), device_id_type=MESH)
+    for other in lines:
+        pl.semaphore_signal(barrier, inc=1, device_id=other, device_id_type=MESH)
     with jax.named_scope("entry"):
-        pl.semaphore_wait(barrier, len(plane) + 6)
+        pl.semaphore_wait(barrier, len(lines))
 
     def lanes(block):
         return pl.ds(pl.multiple_of(block * 512, 512), 512)
@@ -128,9 +126,11 @@
 
     def begin():
         spread(0, 0)
-        for h in range(2):
+        def to_x(h):
             for e in (1, 3, 2):
                 keep(send(own_piece(h, wrap(x + e)), R.at[h, 0, :, x, c], x_s.at[h, e], x_r.at[h, e], dev(x + e, y, z, c)))
+
+        to_x(0)
         for k in range(2):
             for side in range(2):
                 q = (k + side) % 2
@@ -156,7 +156,7 @@
         zero = jnp.zeros((8, 128), jnp.float32)
         cond_pick = lax.fori_loop(0, 128, lambda j, a: jnp.where(cond_no == j, cond[j], a), zero)
         val_pick = lax.fori_loop(0, 32, lambda j, a: jnp.where(val_no == j, val[j], a), zero)
-        D[x * 2 + c] = jnp.where(jnp.right_shift(lane, 4) == x * 2 + c, cond_pick - val_pick, 0.0)
+        D[c * 16 + x] = jnp.where(jnp.right_shift(lane, 4) == x * 2 + c, cond_pick - val_pick, 0.0)
         for h in range(2):
             R[h, 0, :, x, c] = rho[:, 16 * h : 16 * h + 16, columns(x)]
 
@@ -169,9 +169,21 @@
         def _():
             send(FQ.at[0], FQ.at[1], q_s, q_r, dev(x, y, z - 1, c))
 
-        for dy, dx, cc in plane:
-            pos = (0, 1, 3, 2)[dy]
-            send(D.at[x * 2 + c], D.at[pos * 8 + x * 2 + c], d_s, d_r, dev(x + dx, y + dy, z, c + cc))
+        for e in (1, 3, 2):
+            keep(send(D.at[c * 16 + x], D.at[c * 16 + x], d_s.at[0, e], d_r.at[0, e], dev(x + e, y, z, c)))
+        to_x(1)
+
+    def energies_y():
+        for e in (1, 3, 2):
+            arrived(D.at[c * 16 + at(e)], d_r.at[0, e])
+        row = D.at[pl.ds(c * 16, 4)]
+        for dy, pos in ((1, 1), (3, 2), (2, 3)):
+            keep(send(row, D.at[pl.ds(c * 16 + pos * 4, 4)], d_s.at[1, dy], d_r.at[1, dy], dev(x, y + dy, z, c)))
+
+    def energies_core():
+        for dy, pos in ((1, 1), (3, 2), (2, 3)):
+            arrived(D.at[pl.ds(c * 16 + pos * 4, 4)], d_r.at[1, dy])
+        keep(send(D.at[pl.ds(c * 16, 16)], D.at[pl.ds(c * 16, 16)], d_s.at[0, 0], d_r.at[0, 0], partner))
 
     def vectors_pass():
         @pl.when(unaligned)
@@ -220,9 +232,9 @@
         total = C32[h, x, pos]
         for e in (1, 2, 3):
             total = total + CR[h, e, pos].astype(jnp.float32)
-        delta = D[pos * 8]
+        delta = D[pos * 4]
         for k in range(1, 8):
-            delta = delta + D[pos * 8 + k]
+            delta = delta + D[(k // 4) * 16 + pos * 4 + k % 4]
         delta = delta[h : h + 1]
         ratio = delta / (delta * delta + own * own)
         weight = (-4.0 * prefactor * ratio).astype(jnp.bfloat16).astype(jnp.float32)
@@ -275,9 +287,7 @@
                 acc[:, block * 512 : block * 512 + 512] += part
 
     def energies_done():
-        most = D.at[pl.ds(0, 31)]
-        arrived(most, d_r)
-        sent(most, d_s)
+        arrived(D.at[pl.ds((1 - c) * 16, 16)], d_r.at[0, 0])
 
         @pl.when(aligned)
         def _():
@@ -293,6 +303,7 @@
     stage("passA0", pass_on, 0, 0)
     stage("xA2", from_x, 0, 2)
     stage("relay", vectors_pass)
+    stage("energies_y", energies_y)
     stage("passA1", pass_on, 0, 1)
     stage("passA3", pass_on, 0, 3)
     stage("xB1", from_x, 1, 1)
@@ -301,6 +312,7 @@
     stage("passA2", pass_on, 0, 2)
     stage("passB0", pass_on, 1, 0)
     stage("xB2", from_x, 1, 2)
+    stage("energies_core", energies_core)
     stage("vectors", vectors_done)
     stage("partA0", partner_done, 0, 0)
     stage("crossA0", cross, 0, 0)
@@ -528,7 +540,7 @@
             dma((2, 4, 4)), dma((2, 4, 4)),
             dma((2, 4, 4)), dma((2, 4, 4)),
             dma((4, 2)), dma((4, 2)), dma((2, 2)),
-            dma, dma,
+            dma((2, 4)), dma((2, 4)),
             dma((2,)), dma((4,)),
             dma((4, 2)), dma((4,)),
             dma, dma,

time: 85.6 us -> 84.8 us (level)
  no operation moved by 1% of the time
where the time goes in v6:
time: 84.8 us; the launch traced here: 84.6 us
  Pallas kernels  80.1 us (94%)
  local copies, waits for them, and re-layouts  2.59 us (3%)
  other arithmetic  1.18 us (1%)
    pallas_call x1, Pallas kernels, shards(): pl.pallas_call(functools.partial(kernel, (prefactor, grid_count)), name='...  80.1 us
    unnamed x12, local copies, waits for them, and re-layouts  2.59 us

profile of v6, /device:TPU:0, one launch (start us, length us, event | category | flops | bytes accessed | tf_op | source)
XLA Modules:
  0.0 84.6 jit_solution(7071354058104877115)
XLA Ops:
  0.6 0.0 copy-start.1
  0.6 0.0 copy-start.2
  0.7 0.0 copy-start.3
  0.7 0.0 copy-start.4
  0.7 0.0 copy-start
  0.7 1.9 %copy.10 = bf16[32,2,8192]{2,0,1:T(8,128)(2,1)S(1)} copy(bf16[32,2,8192]{2,1,0:T(2,128)(2,1)} %param.6) | data formatting | bytes 2097152 | tf_op args[0]
  2.5 0.0 copy-done.1
  2.6 0.0 copy-done.2
  2.6 0.0 copy-done.3
  2.6 0.0 copy-done.4
  2.6 0.0 copy-done
  2.6 80.1 %response.1 = (bf16[3,2,2,2,64,512]{5,4,3,2,1,0:T(8,128)(2,1)S(1)}, f32[4,2,64,64]{3,2,1,0:T(8,128)S(1)}) custom-call(bf16[2,32,8192]{2,1,0:T(8,128)(2,1)S(1)} %bitcast.4, bf16[4,2,64,512]{3,2,1,0:T(8,128)(2,1)S(1)} %copy-done, s32[32]{0:T(128)S(1)} %copy-done.1, f32[128]{0:T(128)S(1)} %copy-done.2, f32[32]{0:T(128)S(1)} %copy-done.3, f32[4]{0:T(128)S(1)} %copy-done.4), custom_call_target="tpu_custom_call" | custom-call | tf_op jit(solution)/shard_map/response/pallas_call | solution.py:510
  82.7 1.2 %convert_add_fusion = f32[1,2,2,2,64,512]{5,4,3,2,1,0:T(8,128)} fusion(bf16[3,2,2,2,64,512]{5,4,3,2,1,0:T(8,128)(2,1)S(1)} %get-tuple-element.4), kind=kLoop, calls=%fused_computation.1 | loop fusion | flops 1310720 | bytes 2621440 | tf_op jit(solution)/shard_map/add | solution.py:552
  83.9 0.7 copy.12
Async XLA Ops:
  0.6 1.9 %copy-start.1 = (s32[32]{0:T(128)S(1)}, s32[32]{0:T(128)}, u32[]{:S(2)}) copy-start(s32[32]{0:T(128)} %idx.1) | copy-start | bytes 388
  0.6 1.9 %copy-start.2 = (f32[128]{0:T(128)S(1)}, f32[128]{0:T(128)}, u32[]{:S(2)}) copy-start(f32[128]{0:T(128)} %cond.1) | copy-start | bytes 1540
  0.7 1.9 %copy-start.3 = (f32[32]{0:T(128)S(1)}, f32[32]{0:T(128)}, u32[]{:S(2)}) copy-start(f32[32]{0:T(128)} %val.1) | copy-start | bytes 388
  0.7 1.9 %copy-start.4 = (f32[4]{0:T(128)S(1)}, f32[4]{0:T(128)}, u32[]{:S(2)}) copy-start(f32[4]{0:T(128)} %freq.1) | copy-start | bytes 52
  0.7 1.9 %copy-start = (bf16[4,2,64,512]{3,2,1,0:T(8,128)(2,1)S(1)}, bf16[4,2,64,512]{3,2,1,0:T(8,128)(2,1)}, u32[]{:S(2)}) copy-start(bf16[4,2,64,512]{3,2,1,0:T(8,128)(2,1)} %xin.1) | copy-start | bytes 1572868

commit v7 on v6

--- a/solution.py
+++ b/solution.py
@@ -345,12 +345,12 @@
     stage("crossB1", cross, 1, 1)
     stage("outB1", cross_out, 1, 1)
     stage("farB1", pass_far, 1, 1)
+    stage("partB2", partner_done, 1, 2)
+    stage("crossB2", cross, 1, 2)
+    stage("outB2", cross_out, 1, 2)
     stage("farB3", pass_far, 1, 3)
     stage("farB2", pass_far, 1, 2)
     stage("scaleA3", scale, 0, 3)
-    stage("partB2", partner_done, 1, 2)
-    stage("crossB2", cross, 1, 2)
-    stage("outB2", cross_out, 1, 2)
     stage("partB3", partner_done, 1, 3)
     stage("crossB3", cross, 1, 3)
     stage("outB3", cross_out, 1, 3)

time: 84.8 us -> 84.7 us (level)
  no operation moved by 1% of the time
where the time goes in v7:
time: 84.7 us; the launch traced here: 84.6 us
  Pallas kernels  80.1 us (95%)
  local copies, waits for them, and re-layouts  2.59 us (3%)
  other arithmetic  1.18 us (1%)
    pallas_call x1, Pallas kernels, shards(): pl.pallas_call(functools.partial(kernel, (prefactor, grid_count)), name='...  80.1 us
    unnamed x12, local copies, waits for them, and re-layouts  2.59 us

profile of v7, /device:TPU:0, one launch (start us, length us, event | category | flops | bytes accessed | tf_op | source)
XLA Modules:
  0.0 84.6 jit_solution(16388954246569609300)
XLA Ops:
  0.6 0.0 copy-start.1
  0.6 0.0 copy-start.2
  0.7 0.0 copy-start.3
  0.7 0.0 copy-start.4
  0.7 0.0 copy-start
  0.7 1.9 %copy.10 = bf16[32,2,8192]{2,0,1:T(8,128)(2,1)S(1)} copy(bf16[32,2,8192]{2,1,0:T(2,128)(2,1)} %param.6) | data formatting | bytes 2097152 | tf_op args[0]
  2.5 0.0 copy-done.1
  2.6 0.0 copy-done.2
  2.6 0.0 copy-done.3
  2.6 0.0 copy-done.4
  2.6 0.0 copy-done
  2.6 80.1 %response.1 = (bf16[3,2,2,2,64,512]{5,4,3,2,1,0:T(8,128)(2,1)S(1)}, f32[4,2,64,64]{3,2,1,0:T(8,128)S(1)}) custom-call(bf16[2,32,8192]{2,1,0:T(8,128)(2,1)S(1)} %bitcast.4, bf16[4,2,64,512]{3,2,1,0:T(8,128)(2,1)S(1)} %copy-done, s32[32]{0:T(128)S(1)} %copy-done.1, f32[128]{0:T(128)S(1)} %copy-done.2, f32[32]{0:T(128)S(1)} %copy-done.3, f32[4]{0:T(128)S(1)} %copy-done.4), custom_call_target="tpu_custom_call" | custom-call | tf_op jit(solution)/shard_map/response/pallas_call | solution.py:510
  82.7 1.2 %convert_add_fusion = f32[1,2,2,2,64,512]{5,4,3,2,1,0:T(8,128)} fusion(bf16[3,2,2,2,64,512]{5,4,3,2,1,0:T(8,128)(2,1)S(1)} %get-tuple-element.4), kind=kLoop, calls=%fused_computation.1 | loop fusion | flops 1310720 | bytes 2621440 | tf_op jit(solution)/shard_map/add | solution.py:552
  83.9 0.7 copy.12
Async XLA Ops:
  0.6 1.9 %copy-start.1 = (s32[32]{0:T(128)S(1)}, s32[32]{0:T(128)}, u32[]{:S(2)}) copy-start(s32[32]{0:T(128)} %idx.1) | copy-start | bytes 388
  0.6 1.9 %copy-start.2 = (f32[128]{0:T(128)S(1)}, f32[128]{0:T(128)}, u32[]{:S(2)}) copy-start(f32[128]{0:T(128)} %cond.1) | copy-start | bytes 1540
  0.7 1.9 %copy-start.3 = (f32[32]{0:T(128)S(1)}, f32[32]{0:T(128)}, u32[]{:S(2)}) copy-start(f32[32]{0:T(128)} %val.1) | copy-start | bytes 388
  0.7 1.9 %copy-start.4 = (f32[4]{0:T(128)S(1)}, f32[4]{0:T(128)}, u32[]{:S(2)}) copy-start(f32[4]{0:T(128)} %freq.1) | copy-start | bytes 52
  0.7 1.9 %copy-start = (bf16[4,2,64,512]{3,2,1,0:T(8,128)(2,1)S(1)}, bf16[4,2,64,512]{3,2,1,0:T(8,128)(2,1)}, u32[]{:S(2)}) copy-start(bf16[4,2,64,512]{3,2,1,0:T(8,128)(2,1)} %xin.1) | copy-start | bytes 1572868

commit v8 on v7

--- a/solution.py
+++ b/solution.py
@@ -28,8 +28,8 @@
 def kernel(
     consts,
     rho, xin, idx, cond, val, freq,
-    RI, sub,
-    R, XF, acc, C32, CB, CR, SF, L, SB, RC, D, SZ, SO, SA, FQ,
+    RI, SO,
+    R, XF, acc, C32, CB, CR, SF, L, SB, RC, D, SZ, SA, FQ,
     x_s, x_r, y_s, y_r, f_s, f_r, p_s, p_r, v_s, v_r, t_s, c_s, c_r, g_s, g_r,
     i_s, i_r, k_r, d_s, d_r, u_s, u_r, w_s, w_r, q_s, q_r,
 ):
@@ -397,10 +397,6 @@
 
         for e in (1, 3, 2):
             arrived(SO.at[at(e)], w_r.at[e])
-        for f in range(4):
-            both = SO[f]
-            sub[f, 0] = both[:, 0:64]
-            sub[f, 1] = both[:, 64:128]
 
     stage("project_z", project_z)
     stage("imageB", image, B)
@@ -494,6 +490,14 @@
             sent(SO.at[x], w_s.at[0, 0])
 
     stage("drain", drain)
+
+
+def finish(parts, so, img, sub):
+    for f in range(4):
+        total = parts[0, f].astype(jnp.float32) + parts[1, f].astype(jnp.float32)
+        img[f] = total + parts[2, f].astype(jnp.float32)
+        sub[f, 0] = so[f, :, 0:64]
+        sub[f, 1] = so[f, :, 64:128]
 
 
 def shards(pair_density, trial_vectors, frequency, val_energy, cond_energy, pair_index):
@@ -512,7 +516,7 @@
         name="response",
         out_shape=(
             jax.ShapeDtypeStruct((3, 2, 2, 2, 64, 512), bf),
-            jax.ShapeDtypeStruct((4, 2, 64, 64), f32),
+            jax.ShapeDtypeStruct((4, 64, 128), f32),
         ),
         in_specs=[vmem, vmem, smem, smem, smem, smem],
         out_specs=(vmem, vmem),
@@ -528,7 +532,6 @@
             pltpu.VMEM((4, 2, 2, 2, 64, 512), bf),
             pltpu.VMEM((2, 2, 2, 2, 64, 512), bf),
             pltpu.VMEM((32, 8, 128), f32),
-            pltpu.VMEM((4, 64, 128), f32),
             pltpu.VMEM((4, 64, 128), f32),
             pltpu.VMEM((256, 128), f32),
             pltpu.VMEM((2, 4, 8, 128), f32),
@@ -549,8 +552,17 @@
             collective_id=0, has_side_effects=True, vmem_limit_bytes=36 * 2**20
         ),
     )(pieces, trial_vectors, pair_index, cond_energy, val_energy, frequency)
-    images = parts[0].astype(f32) + parts[1].astype(f32) + parts[2].astype(f32)
-    return images.reshape(4, 2, 64, 512), subspace
+    return pl.pallas_call(
+        finish,
+        name="finish",
+        out_shape=(
+            jax.ShapeDtypeStruct((4, 2, 64, 512), f32),
+            jax.ShapeDtypeStruct((4, 2, 64, 64), f32),
+        ),
+        in_specs=[vmem, vmem],
+        out_specs=(vmem, vmem),
+        compiler_params=pltpu.CompilerParams(vmem_limit_bytes=8 * 2**20),
+    )(parts.reshape(3, 4, 2, 64, 512), subspace)
 
 
 def solution(mesh):

time: 84.7 us -> 84.1 us (level)
  Pallas kernels: 80.1 us -> 81.3 us
  other arithmetic: 1.18 us -> 0 us
    pallas_call x0 -> x1, Pallas kernels: none -> 1.23 us  [shards(): pl.pallas_call(finish, name='finish', out_shape=(jax.ShapeDtypeStruct((4,...]
    add x1 -> x0, other arithmetic: 1.18 us -> none  [shards(): images = parts[0].astype(f32) + parts[1].astype(f32) + parts[2].astype(f32)]
    unnamed x12 -> x11, local copies, waits for them, and re-layouts: 2.59 us -> 1.88 us
where the time goes in v8:
time: 84.1 us; the launch traced here: 83.9 us
  Pallas kernels  81.3 us (97%)
  local copies, waits for them, and re-layouts  1.88 us (2%)
    pallas_call x1, Pallas kernels, shards(): pl.pallas_call(functools.partial(kernel, (prefactor, grid_count)), name='...  80.1 us
    unnamed x11, local copies, waits for them, and re-layouts  1.88 us

profile of v8, /device:TPU:0, one launch (start us, length us, event | category | flops | bytes accessed | tf_op | source)
XLA Modules:
  0.0 83.9 jit_solution(4238051776908304288)
XLA Ops:
  0.6 0.0 copy-start.1
  0.6 0.0 copy-start.2
  0.7 0.0 copy-start.3
  0.7 0.0 copy-start.4
  0.7 0.0 copy-start
  0.7 1.9 %copy.10 = bf16[32,2,8192]{2,0,1:T(8,128)(2,1)S(1)} copy(bf16[32,2,8192]{2,1,0:T(2,128)(2,1)} %param.6) | data formatting | bytes 2097152 | tf_op args[0]
  2.5 0.0 copy-done.1
  2.6 0.0 copy-done.2
  2.6 0.0 copy-done.3
  2.6 0.0 copy-done.4
  2.6 0.0 copy-done
  2.6 80.1 %response.1 = (bf16[3,2,2,2,64,512]{5,4,3,2,1,0:T(8,128)(2,1)S(1)}, f32[4,64,128]{2,1,0:T(8,128)S(1)}) custom-call(bf16[2,32,8192]{2,1,0:T(8,128)(2,1)S(1)} %bitcast.4, bf16[4,2,64,512]{3,2,1,0:T(8,128)(2,1)S(1)} %copy-done, s32[32]{0:T(128)S(1)} %copy-done.1, f32[128]{0:T(128)S(1)} %copy-done.2, f32[32]{0:T(128)S(1)} %copy-done.3, f32[4]{0:T(128)S(1)} %copy-done.4), custom_call_target="tpu_custom_call" | custom-call | tf_op jit(solution)/shard_map/response/pallas_call | solution.py:514
  82.7 1.2 %finish.1 = (f32[4,2,64,512]{3,2,1,0:T(8,128)}, f32[4,2,64,64]{3,2,1,0:T(8,128)}) custom-call(bf16[3,4,2,64,512]{4,3,2,1,0:T(8,128)(2,1)S(1)} %bitcast.5, f32[4,64,128]{2,1,0:T(8,128)S(1)} %get-tuple-element.5.so), custom_call_target="tpu_custom_call" | custom-call | tf_op jit(solution)/shard_map/finish/pallas_call | solution.py:555
Async XLA Ops:
  0.6 1.9 %copy-start.1 = (s32[32]{0:T(128)S(1)}, s32[32]{0:T(128)}, u32[]{:S(2)}) copy-start(s32[32]{0:T(128)} %idx.1) | copy-start | bytes 388
  0.6 1.9 %copy-start.2 = (f32[128]{0:T(128)S(1)}, f32[128]{0:T(128)}, u32[]{:S(2)}) copy-start(f32[128]{0:T(128)} %cond.1) | copy-start | bytes 1540
  0.7 1.9 %copy-start.3 = (f32[32]{0:T(128)S(1)}, f32[32]{0:T(128)}, u32[]{:S(2)}) copy-start(f32[32]{0:T(128)} %val.1) | copy-start | bytes 388
  0.7 1.9 %copy-start.4 = (f32[4]{0:T(128)S(1)}, f32[4]{0:T(128)}, u32[]{:S(2)}) copy-start(f32[4]{0:T(128)} %freq.1) | copy-start | bytes 52
  0.7 1.9 %copy-start = (bf16[4,2,64,512]{3,2,1,0:T(8,128)(2,1)S(1)}, bf16[4,2,64,512]{3,2,1,0:T(8,128)(2,1)}, u32[]{:S(2)}) copy-start(bf16[4,2,64,512]{3,2,1,0:T(8,128)(2,1)} %xin.1) | copy-start | bytes 1572868

commit v9 on v8

--- a/solution.py
+++ b/solution.py
@@ -354,11 +354,11 @@
     stage("partB3", partner_done, 1, 3)
     stage("crossB3", cross, 1, 3)
     stage("outB3", cross_out, 1, 3)
+    stage("imageA", image, A)
     stage("scaleB1", scale, 1, 1)
-    stage("imageA", image, A)
     stage("scaleB2", scale, 1, 2)
+    stage("imageF", image, FAR)
     stage("scaleB3", scale, 1, 3)
-    stage("imageF", image, FAR)
     stage("addA", project_add, A)
     stage("addF", project_add, FAR)
     stage("addB", project_add, B)
@@ -492,12 +492,19 @@
     stage("drain", drain)
 
 
-def finish(parts, so, img, sub):
+def finish(parts, so, img, sub, images, matrix, i_sem, m_sem):
+    for f in range(4):
+        matrix[f, 0] = so[f, :, 0:64]
+        matrix[f, 1] = so[f, :, 64:128]
+    copies = [pltpu.make_async_copy(matrix, sub, m_sem)]
+    copies[0].start()
     for f in range(4):
         total = parts[0, f].astype(jnp.float32) + parts[1, f].astype(jnp.float32)
-        img[f] = total + parts[2, f].astype(jnp.float32)
-        sub[f, 0] = so[f, :, 0:64]
-        sub[f, 1] = so[f, :, 64:128]
+        images[f] = total + parts[2, f].astype(jnp.float32)
+        copies.append(pltpu.make_async_copy(images.at[f], img.at[f], i_sem.at[f]))
+        copies[-1].start()
+    for copy in copies:
+        copy.wait()
 
 
 def shards(pair_density, trial_vectors, frequency, val_energy, cond_energy, pair_index):
@@ -510,6 +517,7 @@
     bf, f32 = jnp.bfloat16, jnp.float32
     vmem = pl.BlockSpec(memory_space=pltpu.VMEM)
     smem = pl.BlockSpec(memory_space=pltpu.SMEM)
+    hbm = pl.BlockSpec(memory_space=pltpu.HBM)
     dma = pltpu.SemaphoreType.DMA
     parts, subspace = pl.pallas_call(
         functools.partial(kernel, (prefactor, grid_count)),
@@ -560,7 +568,12 @@
             jax.ShapeDtypeStruct((4, 2, 64, 64), f32),
         ),
         in_specs=[vmem, vmem],
-        out_specs=(vmem, vmem),
+        out_specs=(hbm, hbm),
+        scratch_shapes=[
+            pltpu.VMEM((4, 2, 64, 512), f32),
+            pltpu.VMEM((4, 2, 64, 64), f32),
+            dma((4,)), dma,
+        ],
         compiler_params=pltpu.CompilerParams(vmem_limit_bytes=8 * 2**20),
     )(parts.reshape(3, 4, 2, 64, 512), subspace)
 

time: 84.1 us -> 83.9 us (level)
  no operation moved by 1% of the time
where the time goes in v9:
time: 83.9 us; the launch traced here: 83.8 us
  Pallas kernels  81.2 us (97%)
  local copies, waits for them, and re-layouts  1.88 us (2%)
    pallas_call x1, Pallas kernels, shards(): pl.pallas_call(functools.partial(kernel, (prefactor, grid_count)), name='...  80 us
    unnamed x11, local copies, waits for them, and re-layouts  1.88 us

profile of v9, /device:TPU:0, one launch (start us, length us, event | category | flops | bytes accessed | tf_op | source)
XLA Modules:
  0.0 83.8 jit_solution(12912111023677593203)
XLA Ops:
  0.6 0.0 copy-start.1
  0.6 0.0 copy-start.2
  0.7 0.0 copy-start.3
  0.7 0.0 copy-start.4
  0.7 0.0 copy-start
  0.7 1.9 %copy.10 = bf16[32,2,8192]{2,0,1:T(8,128)(2,1)S(1)} copy(bf16[32,2,8192]{2,1,0:T(2,128)(2,1)} %param.6) | data formatting | bytes 2097152 | tf_op args[0]
  2.5 0.0 copy-done.1
  2.6 0.0 copy-done.2
  2.6 0.0 copy-done.3
  2.6 0.0 copy-done.4
  2.6 0.0 copy-done
  2.6 80.0 %response.1 = (bf16[3,2,2,2,64,512]{5,4,3,2,1,0:T(8,128)(2,1)S(1)}, f32[4,64,128]{2,1,0:T(8,128)S(1)}) custom-call(bf16[2,32,8192]{2,1,0:T(8,128)(2,1)S(1)} %bitcast.4, bf16[4,2,64,512]{3,2,1,0:T(8,128)(2,1)S(1)} %copy-done, s32[32]{0:T(128)S(1)} %copy-done.1, f32[128]{0:T(128)S(1)} %copy-done.2, f32[32]{0:T(128)S(1)} %copy-done.3, f32[4]{0:T(128)S(1)} %copy-done.4), custom_call_target="tpu_custom_call" | custom-call | tf_op jit(solution)/shard_map/response/pallas_call | solution.py:522
  82.6 1.2 %finish.1 = (f32[4,2,64,512]{3,2,1,0:T(8,128)}, f32[4,2,64,64]{3,2,1,0:T(8,128)}) custom-call(bf16[3,4,2,64,512]{4,3,2,1,0:T(8,128)(2,1)S(1)} %bitcast.5, f32[4,64,128]{2,1,0:T(8,128)S(1)} %get-tuple-element.5.so), custom_call_target="tpu_custom_call" | custom-call | tf_op jit(solution)/shard_map/finish/pallas_call | solution.py:563
Async XLA Ops:
  0.6 1.9 %copy-start.1 = (s32[32]{0:T(128)S(1)}, s32[32]{0:T(128)}, u32[]{:S(2)}) copy-start(s32[32]{0:T(128)} %idx.1) | copy-start | bytes 388
  0.6 1.9 %copy-start.2 = (f32[128]{0:T(128)S(1)}, f32[128]{0:T(128)}, u32[]{:S(2)}) copy-start(f32[128]{0:T(128)} %cond.1) | copy-start | bytes 1540
  0.7 1.9 %copy-start.3 = (f32[32]{0:T(128)S(1)}, f32[32]{0:T(128)}, u32[]{:S(2)}) copy-start(f32[32]{0:T(128)} %val.1) | copy-start | bytes 388
  0.7 1.9 %copy-start.4 = (f32[4]{0:T(128)S(1)}, f32[4]{0:T(128)}, u32[]{:S(2)}) copy-start(f32[4]{0:T(128)} %freq.1) | copy-start | bytes 52
  0.7 1.9 %copy-start = (bf16[4,2,64,512]{3,2,1,0:T(8,128)(2,1)S(1)}, bf16[4,2,64,512]{3,2,1,0:T(8,128)(2,1)}, u32[]{:S(2)}) copy-start(bf16[4,2,64,512]{3,2,1,0:T(8,128)(2,1)} %xin.1) | copy-start | bytes 1572868

commit v10 on v9

--- a/solution.py
+++ b/solution.py
@@ -354,11 +354,11 @@
     stage("partB3", partner_done, 1, 3)
     stage("crossB3", cross, 1, 3)
     stage("outB3", cross_out, 1, 3)
+    stage("scaleB1", scale, 1, 1)
     stage("imageA", image, A)
-    stage("scaleB1", scale, 1, 1)
     stage("scaleB2", scale, 1, 2)
+    stage("scaleB3", scale, 1, 3)
     stage("imageF", image, FAR)
-    stage("scaleB3", scale, 1, 3)
     stage("addA", project_add, A)
     stage("addF", project_add, FAR)
     stage("addB", project_add, B)

time: 83.9 us -> 84 us (level)
  no operation moved by 1% of the time
where the time goes in v10:
time: 84 us; the launch traced here: 83.9 us
  Pallas kernels  81.3 us (97%)
  local copies, waits for them, and re-layouts  1.88 us (2%)
    pallas_call x1, Pallas kernels, shards(): pl.pallas_call(functools.partial(kernel, (prefactor, grid_count)), name='...  80.1 us
    unnamed x11, local copies, waits for them, and re-layouts  1.88 us

profile of v10, /device:TPU:0, one launch (start us, length us, event | category | flops | bytes accessed | tf_op | source)
XLA Modules:
  0.0 83.9 jit_solution(273745002963047647)
XLA Ops:
  0.6 0.0 copy-start.1
  0.6 0.0 copy-start.2
  0.7 0.0 copy-start.3
  0.7 0.0 copy-start.4
  0.7 0.0 copy-start
  0.7 1.9 %copy.10 = bf16[32,2,8192]{2,0,1:T(8,128)(2,1)S(1)} copy(bf16[32,2,8192]{2,1,0:T(2,128)(2,1)} %param.6) | data formatting | bytes 2097152 | tf_op args[0]
  2.5 0.0 copy-done.1
  2.6 0.0 copy-done.2
  2.6 0.0 copy-done.3
  2.6 0.0 copy-done.4
  2.6 0.0 copy-done
  2.6 80.1 %response.1 = (bf16[3,2,2,2,64,512]{5,4,3,2,1,0:T(8,128)(2,1)S(1)}, f32[4,64,128]{2,1,0:T(8,128)S(1)}) custom-call(bf16[2,32,8192]{2,1,0:T(8,128)(2,1)S(1)} %bitcast.4, bf16[4,2,64,512]{3,2,1,0:T(8,128)(2,1)S(1)} %copy-done, s32[32]{0:T(128)S(1)} %copy-done.1, f32[128]{0:T(128)S(1)} %copy-done.2, f32[32]{0:T(128)S(1)} %copy-done.3, f32[4]{0:T(128)S(1)} %copy-done.4), custom_call_target="tpu_custom_call" | custom-call | tf_op jit(solution)/shard_map/response/pallas_call | solution.py:522
  82.7 1.2 %finish.1 = (f32[4,2,64,512]{3,2,1,0:T(8,128)}, f32[4,2,64,64]{3,2,1,0:T(8,128)}) custom-call(bf16[3,4,2,64,512]{4,3,2,1,0:T(8,128)(2,1)S(1)} %bitcast.5, f32[4,64,128]{2,1,0:T(8,128)S(1)} %get-tuple-element.5.so), custom_call_target="tpu_custom_call" | custom-call | tf_op jit(solution)/shard_map/finish/pallas_call | solution.py:563
Async XLA Ops:
  0.6 1.9 %copy-start.1 = (s32[32]{0:T(128)S(1)}, s32[32]{0:T(128)}, u32[]{:S(2)}) copy-start(s32[32]{0:T(128)} %idx.1) | copy-start | bytes 388
  0.6 1.9 %copy-start.2 = (f32[128]{0:T(128)S(1)}, f32[128]{0:T(128)}, u32[]{:S(2)}) copy-start(f32[128]{0:T(128)} %cond.1) | copy-start | bytes 1540
  0.7 1.9 %copy-start.3 = (f32[32]{0:T(128)S(1)}, f32[32]{0:T(128)}, u32[]{:S(2)}) copy-start(f32[32]{0:T(128)} %val.1) | copy-start | bytes 388
  0.7 1.9 %copy-start.4 = (f32[4]{0:T(128)S(1)}, f32[4]{0:T(128)}, u32[]{:S(2)}) copy-start(f32[4]{0:T(128)} %freq.1) | copy-start | bytes 52
  0.7 1.9 %copy-start = (bf16[4,2,64,512]{3,2,1,0:T(8,128)(2,1)S(1)}, bf16[4,2,64,512]{3,2,1,0:T(8,128)(2,1)}, u32[]{:S(2)}) copy-start(bf16[4,2,64,512]{3,2,1,0:T(8,128)(2,1)} %xin.1) | copy-start | bytes 1572868
